TPU v7x, 32 devices: a whole 2x2x4 slice. The times are simulated.
32 devices in a mesh: sub: 16 (over z, x, core), rng: 2 (over y).
Axes of the slice: x: 2, y: 2, z: 4, core: 2. Of those that a mesh axis runs over, the one named last changes fastest.
Arguments:
- raw_echoes: bfloat16 [2, 4096, 4096], P(None, ('sub', 'rng')), may hold values from -6 to 6
- merge_taps: int32 [4, 2, 8, 512], replicated, may hold values from 0 to 255
- merge_weights: float32 [4, 2, 8, 512], replicated, may hold values from -2 to 2
- track_offsets: int32 [4, 16], replicated, may hold values from 0 to 63
Outputs:
- despeckled: float32 [4096, 4096], P('sub', 'rng')
All inputs are finite; a program needn't handle non-finite values.
Results may differ from a plain program's by a relative error of at most 0.0045.
Values may be sent and summed in bfloat16 or wider, within the bound.
No kernel may reach another device: no remote copies, remote signals or barrier semaphores. Data moves between devices by JAX's collectives and lax.ppermute only.
A program may use at most 64 MiB of HBM per device.

v0:
```python
import math

import jax
import jax.numpy as jnp
from jax import lax
from jax.sharding import PartitionSpec as P

FACTOR = 64
ANG = 256
MERGES = 4
SWEEPS = 8


inv_root_two = 0.7071067811865476
diffusion_rate = 0.5
edge_scale = 2.0
phase_period = 8192


def swapped(array, axis, stride):
    return lax.ppermute(array, axis, [(i, i ^ 1 << stride) for i in range(lax.axis_size(axis))])


def extended(cells, sides, width):
    for axis, dim in sides:
        count = lax.axis_size(axis)
        ends = count - 1
        head = lax.slice_in_dim(cells, 0, width, axis=dim)
        tail = lax.slice_in_dim(cells, cells.shape[dim] - width, cells.shape[dim], axis=dim)
        cells = jnp.concatenate(
            [
                lax.ppermute(tail, axis, [(i, (i + 1) % count) for i in range(ends)]),
                cells,
                lax.ppermute(head, axis, [((i + 1) % count, i) for i in range(ends)]),
            ],
            axis=dim,
        )
    return cells


def complex_mix(real_in, imag_in, cosine_table, sine_table, form):
    highest = lax.Precision.HIGHEST
    real_out = jnp.einsum(form, real_in, cosine_table, precision=highest) + jnp.einsum(
        form, imag_in, sine_table, precision=highest
    )
    imag_out = jnp.einsum(form, imag_in, cosine_table, precision=highest) - jnp.einsum(
        form, real_in, sine_table, precision=highest
    )
    return (real_out, imag_out)


def range_transform(raw_block, factor):
    row_count = raw_block.shape[1]
    samples_all = factor * factor
    samples_in = raw_block.astype(jnp.float32).reshape(2, row_count, factor, factor)
    sample_index = jnp.arange(factor, dtype=jnp.int32)
    product = sample_index[:, None] * sample_index[None, :]
    coarse = 2.0 * math.pi / factor * (product % factor).astype(jnp.float32)
    twiddle = 2.0 * math.pi / samples_all * (product % samples_all).astype(jnp.float32)
    cosine_table = jnp.cos(coarse)
    sine_table = jnp.sin(coarse)
    first_real, first_imag = complex_mix(
        samples_in[0], samples_in[1], cosine_table, sine_table, "pab,ac->pbc"
    )
    twist_cos = jnp.cos(twiddle)
    twist_sin = jnp.sin(twiddle)
    second_real = first_real * twist_cos + first_imag * twist_sin
    second_imag = first_imag * twist_cos - first_real * twist_sin
    final_real, final_imag = complex_mix(
        second_real, second_imag, cosine_table, sine_table, "pbc,bd->pdc"
    )
    norm_scale = 1.0 / factor
    return jnp.stack([final_real, final_imag]).reshape(2, row_count, samples_all) * norm_scale


def beam_tables(angle_count, leaf_pulses):
    angle_index = jnp.arange(angle_count, dtype=jnp.int32) - angle_count // 2
    pulse_index = jnp.arange(leaf_pulses, dtype=jnp.int32)
    wrapped = angle_index[:, None] * pulse_index[None, :] % leaf_pulses
    angles_now = 2.0 * math.pi / leaf_pulses * wrapped.astype(jnp.float32)
    norm_scale = 1.0 / math.sqrt(leaf_pulses)
    return (
        (jnp.cos(angles_now) * norm_scale).astype(jnp.bfloat16),
        (jnp.sin(angles_now) * norm_scale).astype(jnp.bfloat16),
    )


def form_leaf(compressed, cosine_table, sine_table):
    real_part = jnp.dot(cosine_table, compressed[0], preferred_element_type=jnp.float32) + jnp.dot(
        sine_table, compressed[1], preferred_element_type=jnp.float32
    )
    imag_part = jnp.dot(cosine_table, compressed[1], preferred_element_type=jnp.float32) - jnp.dot(
        sine_table, compressed[0], preferred_element_type=jnp.float32
    )
    return jnp.stack([real_part, imag_part]).astype(jnp.bfloat16)


def interp_matrix(taps_rows, weights_rows, angle_count):
    columns = jnp.arange(angle_count, dtype=jnp.int32)
    summed = jnp.zeros((taps_rows.shape[1], angle_count), jnp.float32)
    for tap_index in range(taps_rows.shape[0]):
        summed = summed + jnp.where(
            taps_rows[tap_index][:, None] == columns[None, :], weights_rows[tap_index][:, None], 0.0
        )
    return summed.astype(jnp.bfloat16)


def contribute(sector_image, matrix, offset, row_anchor, col_anchor):
    proj_real = jnp.dot(matrix, sector_image[0], preferred_element_type=jnp.float32)
    proj_imag = jnp.dot(matrix, sector_image[1], preferred_element_type=jnp.float32)
    row_index = row_anchor + jnp.arange(matrix.shape[0], dtype=jnp.int32)
    col_index = col_anchor + 1 + jnp.arange(sector_image.shape[2], dtype=jnp.int32)
    wrapped = (offset * row_index % phase_period)[:, None] * col_index[None, :] % phase_period
    motion_phase = 2.0 * math.pi / phase_period * wrapped.astype(jnp.float32)
    cosine_now = jnp.cos(motion_phase)
    sine_now = jnp.sin(motion_phase)
    return jnp.stack(
        [
            proj_real * cosine_now - proj_imag * sine_now,
            proj_real * sine_now + proj_imag * cosine_now,
        ]
    )


def conduct(difference):
    scaled = difference / edge_scale
    return 1.0 / (1.0 + scaled * scaled)


def diffuse(padded):
    center = padded[:, 1:-1]
    upper_diff = padded[:, 2:] - center
    lower_diff = center - padded[:, :-2]
    return center + diffusion_rate * (
        conduct(upper_diff) * upper_diff - conduct(lower_diff) * lower_diff
    )


def mirror_ends(padded, intensity, margin, position, rng_count):
    lower_part = jnp.where(
        position == 0, jnp.flip(intensity[:, :margin], axis=1), padded[:, :margin]
    )
    upper_part = jnp.where(
        position == rng_count - 1, jnp.flip(intensity[:, -margin:], axis=1), padded[:, -margin:]
    )
    return jnp.concatenate([lower_part, padded[:, margin:-margin], upper_part], axis=1)


def per_device(raw_echoes, merge_taps, merge_weights, track_offsets):
    compressed = range_transform(raw_echoes, FACTOR).astype(jnp.bfloat16)
    regrouped = lax.all_to_all(compressed, "rng", split_axis=2, concat_axis=1, tiled=True)
    leaf_pulses = regrouped.shape[1]
    col_count = regrouped.shape[2]
    cosine_table, sine_table = beam_tables(ANG, leaf_pulses)
    sector_image = form_leaf(regrouped, cosine_table, sine_table)
    leaf_index = lax.axis_index("sub")
    position = lax.axis_index("rng")
    rng_count = lax.axis_size("rng")
    col_anchor = position * col_count
    sector_now = jnp.int32(0)
    for merge_level in range(MERGES):
        partner_bit = 1 << merge_level
        half_bit = leaf_index >> merge_level & 1
        partner_leaf = leaf_index ^ partner_bit
        taps_level = merge_taps[merge_level]
        weights_level = merge_weights[merge_level]
        offset = lax.dynamic_index_in_dim(track_offsets[merge_level], leaf_index, 0, keepdims=False)
        row_anchor = sector_now * (2 * ANG)
        own_taps = lax.dynamic_index_in_dim(taps_level, half_bit, 0, keepdims=False)
        own_weights = lax.dynamic_index_in_dim(weights_level, half_bit, 0, keepdims=False)
        arrived = swapped(sector_image, "sub", merge_level)
        partner_taps = lax.dynamic_index_in_dim(taps_level, 1 - half_bit, 0, keepdims=False)
        partner_weights = lax.dynamic_index_in_dim(weights_level, 1 - half_bit, 0, keepdims=False)
        partner_offset = lax.dynamic_index_in_dim(
            track_offsets[merge_level], partner_leaf, 0, keepdims=False
        )
        half_anchor = half_bit * ANG
        own_rows = interp_matrix(
            lax.dynamic_slice_in_dim(own_taps, half_anchor, ANG, 1),
            lax.dynamic_slice_in_dim(own_weights, half_anchor, ANG, 1),
            ANG,
        )
        partner_rows = interp_matrix(
            lax.dynamic_slice_in_dim(partner_taps, half_anchor, ANG, 1),
            lax.dynamic_slice_in_dim(partner_weights, half_anchor, ANG, 1),
            ANG,
        )
        merged = contribute(
            sector_image, own_rows, offset, row_anchor + half_anchor, col_anchor
        ) + contribute(arrived, partner_rows, partner_offset, row_anchor + half_anchor, col_anchor)
        sector_image = (merged * inv_root_two).astype(jnp.bfloat16)
        sector_now = sector_now * 2 + half_bit
    real_part = sector_image[0].astype(jnp.float32)
    imag_part = sector_image[1].astype(jnp.float32)
    intensity = jnp.sqrt(real_part * real_part + imag_part * imag_part)
    for sweep_index in range(SWEEPS):
        padded = extended(intensity, (("rng", 1),), 1)
        padded = mirror_ends(padded, intensity, 1, position, rng_count)
        intensity = diffuse(padded)
    return intensity


def solution(mesh):
    in_specs = (P(None, ("sub", "rng"), None), P(), P(), P())
    out_specs = P("sub", "rng")
    return jax.shard_map(
        per_device, mesh=mesh, in_specs=in_specs, out_specs=out_specs, check_vma=False
    )
```

profile of v0, /device:TPU:0, one launch (start us, length us, event | category | flops | bytes accessed | tf_op | source)
XLA Modules:
  0.0 459.8 jit_solution(9666238544721001321)
XLA Ops:
  0.3 1.7 fusion.203
  3.3 1.5 fusion.95
  4.9 1.5 fusion.99
  6.4 1.6 convolution_add_fusion.1
  8.0 2.7 fusion.51
  10.7 3.1 fusion.53
  13.8 14.0 %fusion.55 = f32[64,128,64]{1,0,2:T(8,128)S(1)} fusion(f32[128,64,64]{0,2,1:T(8,128)S(1)} %get-tuple-element.6), kind=kOutput, calls=%fused_computation.150 | convolution fusion | flops 402710528 | bytes 4194304 | tf_op jit(solution)/shard_map/pbc,bd->pdc/dot_general | solution.py:43
  27.8 3.2 add_bitcast_fusion.8
  31.0 3.2 subtract_bitcast_fusion.8
  37.0 18.1 %copy.55 = bf16[2,128,4096]{1,0,2:T(2,128)(2,1)} copy(bf16[2,128,4096]{1,2,0:T(8,128)(2,1)S(1)} %fusion) | data formatting | bytes 4194304 | tf_op jit(solution)/shard_map/convert_element_type | solution.py:150
  55.1 4.3 all-to-all-start
  59.4 25.9 %all-to-all-done = bf16[2,128,4096]{1,0,2:T(2,128)(2,1)S(1)} async-done(((bf16[2,128,4096]{1,0,2:T(2,128)(2,1)}), bf16[2,128,4096]{1,0,2:T(2,128)(2,1)S(1)}, u32[]{:S(2)}, u32[]{:S(2)}) %all-to-all-start) | async-done | bytes 2097184 | tf_op jit(solution)/shard_map/all_to_all | solution.py:151
  87.1 1.4 fusion.107
  88.6 1.4 fusion.108
  90.0 1.5 fusion.10
  91.5 1.5 fusion.9
  93.0 1.5 pad_maximum_fusion.16
  99.0 2.2 fusion.78
  101.2 19.4 %subtract_bitcast_fusion.6 = (f32[1,256,2048]{2,1,0:T(8,128)S(1)}, f32[1,256,2048]{2,1,0:T(8,128)S(1)}, f32[1,256,2048]{2,1,0:T(8,128)S(1)}, f32[1,256,2048]{2,1,0:T(8,128)S(1)}) fusion(f32[256,2048]{1,0:T(8,128)S(1)} %fusion.78, s32[2048]{0:T(1024)S(1)} %iota_add_fusion, s32[256]{0:T(256)S(1)} %get-tuple-element.223, f32[256,2048]{1,0:T(8,128)S(1)} %fusion.192, ...), kind=kOutput, calls=%fused_computation.143 | convolution fusion | flops 290979840 | bytes 15755264 | tf_op jit(solution)/shard_map/dot_general | solution.py:110
  121.6 1.8 collective-permute-start.1
  127.1 42.4 %collective-permute-done.1 = bf16[2,256,2048]{2,1,0:T(8,128)(2,1)} collective-permute-done((bf16[2,256,2048]{2,1,0:T(8,128)(2,1)S(1)}, bf16[2,256,2048]{2,1,0:T(8,128)(2,1)}, u32[]{:S(2)}, u32[]{:S(2)}) %collective-permute-start.1) | collective-permute-done | bytes 2097184 | tf_op jit(solution)/shard_map/ppermute | solution.py:21
  169.5 2.2 fusion.74
  171.7 19.6 %subtract_bitcast_fusion.4 = (f32[1,256,2048]{2,1,0:T(8,128)S(1)}, f32[1,256,2048]{2,1,0:T(8,128)S(1)}, f32[1,256,2048]{2,1,0:T(8,128)S(1)}, f32[1,256,2048]{2,1,0:T(8,128)S(1)}) fusion(f32[256,2048]{1,0:T(8,128)S(1)} %fusion.74, s32[2048]{0:T(1024)S(1)} %iota_add_fusion, s32[256]{0:T(256)S(1)} %get-tuple-element.221, f32[256,2048]{1,0:T(8,128)S(1)} %fusion.75, ...), kind=kOutput, calls=%fused_computation.139 | convolution fusion | flops 290979840 | bytes 15755264 | tf_op jit(solution)/shard_map/dot_general | solution.py:110
  192.3 1.9 collective-permute-start.2
  198.3 41.1 %collective-permute-done.2 = bf16[2,256,2048]{2,1,0:T(8,128)(2,1)} collective-permute-done((bf16[2,256,2048]{2,1,0:T(8,128)(2,1)S(1)}, bf16[2,256,2048]{2,1,0:T(8,128)(2,1)}, u32[]{:S(2)}, u32[]{:S(2)}) %collective-permute-start.2) | collective-permute-done | bytes 2097184 | tf_op jit(solution)/shard_map/ppermute | solution.py:21
  239.4 2.2 fusion.70
  241.6 19.2 %subtract_bitcast_fusion.2 = (f32[1,256,2048]{2,1,0:T(8,128)S(1)}, f32[1,256,2048]{2,1,0:T(8,128)S(1)}, f32[1,256,2048]{2,1,0:T(8,128)S(1)}, f32[1,256,2048]{2,1,0:T(8,128)S(1)}) fusion(f32[256,2048]{1,0:T(8,128)S(1)} %fusion.70, s32[2048]{0:T(1024)S(1)} %iota_add_fusion, s32[256]{0:T(256)S(1)} %get-tuple-element.219, f32[256,2048]{1,0:T(8,128)S(1)} %fusion.71, ...), kind=kOutput, calls=%fused_computation.135 | convolution fusion | flops 290979840 | bytes 15755264 | tf_op jit(solution)/shard_map/dot_general | solution.py:110
  260.8 1.4 fusion.6
  262.3 2.8 collective-permute-start.3
  268.8 85.6 %collective-permute-done.3 = bf16[2,256,2048]{2,1,0:T(8,128)(2,1)} collective-permute-done((bf16[2,256,2048]{2,1,0:T(8,128)(2,1)S(1)}, bf16[2,256,2048]{2,1,0:T(8,128)(2,1)}, u32[]{:S(2)}, u32[]{:S(2)}) %collective-permute-start.3) | collective-permute-done | bytes 2097184 | tf_op jit(solution)/shard_map/ppermute | solution.py:21
  354.5 2.2 fusion.66
  356.6 19.2 %subtract_bitcast_fusion = (f32[1,256,2048]{2,1,0:T(8,128)S(1)}, f32[1,256,2048]{2,1,0:T(8,128)S(1)}, f32[1,256,2048]{2,1,0:T(8,128)S(1)}, f32[1,256,2048]{2,1,0:T(8,128)S(1)}) fusion(f32[256,2048]{1,0:T(8,128)S(1)} %fusion.66, s32[2048]{0:T(1024)S(1)} %iota_add_fusion, s32[256]{0:T(256)S(1)} %get-tuple-element.217, f32[256,2048]{1,0:T(8,128)S(1)} %fusion.67, ...), kind=kOutput, calls=%fused_computation.131 | convolution fusion | flops 290979840 | bytes 15755264 | tf_op jit(solution)/shard_map/dot_general | solution.py:110
  377.8 1.3 collective-permute-start.4
  379.1 4.8 %collective-permute-start.5 = (f32[256,1]{1,0:T(8,128)S(1)}, f32[256,1]{1,0:T(8,128)S(1)}, u32[]{:S(2)}, u32[]{:S(2)}) collective-permute-start(f32[256,1]{1,0:T(8,128)S(1)} %get-tuple-element.54), channel_id=1, source_target_pairs={{0,1},{2,3},{4,5},{6,7},{8,9},{10,11},{12,13},{14,15},{16,17},{18,... | collective-permute-start | bytes 3080 | tf_op jit(solution)/shard_map/ppermute | solution.py:32
  384.6 1.5 collective-permute-done.5
  386.2 1.3 multiply_add_fusion.7
  387.6 1.3 collective-permute-start.6
  388.9 4.6 collective-permute-start.7
  394.5 1.5 collective-permute-done.7
  396.1 1.3 multiply_add_fusion.6
  397.5 1.3 collective-permute-start.8
  398.8 4.6 collective-permute-start.9
  404.3 1.5 collective-permute-done.9
  405.9 1.3 multiply_add_fusion.5
  407.3 1.3 collective-permute-start.10
  408.6 4.6 collective-permute-start.11
  414.2 1.5 collective-permute-done.11
  415.8 1.3 multiply_add_fusion.4
  417.2 1.3 collective-permute-start.12
  418.5 4.6 collective-permute-start.13
  424.0 1.5 collective-permute-done.13
  425.6 1.3 multiply_add_fusion.3
  427.0 1.3 collective-permute-start.14
  428.3 4.6 collective-permute-start.15
  432.9 1.4 collective-permute-done.14
  434.3 1.7 collective-permute-done.15
  436.1 1.3 multiply_add_fusion.2
  437.5 1.3 collective-permute-start.16
  438.8 4.6 collective-permute-start.17
  443.4 2.3 collective-permute-done.16
  448.3 1.3 collective-permute-start.18
  449.6 4.6 collective-permute-start.19
  455.2 1.5 collective-permute-done.19
  456.8 2.6 multiply_add_fusion
  (73 shorter events, 36.1 us)
Async XLA Ops:
  55.1 30.1 %all-to-all-start = ((bf16[2,128,4096]{1,0,2:T(2,128)(2,1)}), bf16[2,128,4096]{1,0,2:T(2,128)(2,1)S(1)}, u32[]{:S(2)}, u32[]{:S(2)}) async-start(bf16[2,128,4096]{1,0,2:T(2,128)(2,1)} %copy.55), calls=%async_computation | async-start | bytes 4194304 | tf_op jit(solution)/shard_map/all_to_all | solution.py:151
  92.9 1.5 copy-start.2
  92.9 3.3 copy-start
  92.9 3.6 copy-start.1
  94.5 4.5 collective-permute-start
  121.6 48.0 %collective-permute-start.1 = (bf16[2,256,2048]{2,1,0:T(8,128)(2,1)S(1)}, bf16[2,256,2048]{2,1,0:T(8,128)(2,1)}, u32[]{:S(2)}, u32[]{:S(2)}) collective-permute-start(bf16[2,256,2048]{2,1,0:T(8,128)(2,1)S(1)} %fusion.2), channel_id=1, source_target_pairs={{0,4},{2,6},{4,0},{6,2},{8,12},{10,14},{12,8},{14,10},{16,20},{18,... | collective-permute-start | bytes 6291464 | tf_op jit(solution)/shard_map/ppermute | solution.py:21
  192.3 47.1 %collective-permute-start.2 = (bf16[2,256,2048]{2,1,0:T(8,128)(2,1)S(1)}, bf16[2,256,2048]{2,1,0:T(8,128)(2,1)}, u32[]{:S(2)}, u32[]{:S(2)}) collective-permute-start(bf16[2,256,2048]{2,1,0:T(8,128)(2,1)S(1)} %fusion.4), channel_id=1, source_target_pairs={{0,8},{2,10},{4,12},{6,14},{8,0},{10,2},{12,4},{14,6},{16,24},{18,... | collective-permute-start | bytes 6291464 | tf_op jit(solution)/shard_map/ppermute | solution.py:21
  262.3 92.2 %collective-permute-start.3 = (bf16[2,256,2048]{2,1,0:T(8,128)(2,1)S(1)}, bf16[2,256,2048]{2,1,0:T(8,128)(2,1)}, u32[]{:S(2)}, u32[]{:S(2)}) collective-permute-start(bf16[2,256,2048]{2,1,0:T(8,128)(2,1)S(1)} %fusion.6), channel_id=1, source_target_pairs={{0,16},{2,18},{4,20},{6,22},{8,24},{10,26},{12,28},{14,30},{16,0},... | collective-permute-start | bytes 6291464 | tf_op jit(solution)/shard_map/ppermute | solution.py:21
  377.8 6.9 %collective-permute-start.4 = (f32[256,1]{1,0:T(8,128)S(1)}, f32[256,1]{1,0:T(8,128)S(1)}, u32[]{:S(2)}, u32[]{:S(2)}) collective-permute-start(f32[256,1]{1,0:T(8,128)S(1)} %get-tuple-element.53), channel_id=1, source_target_pairs={{1,0},{3,2},{5,4},{7,6},{9,8},{11,10},{13,12},{15,14},{17,16},{19,... | collective-permute-start | bytes 3080 | tf_op jit(solution)/shard_map/ppermute | solution.py:34
  379.1 7.1 %collective-permute-start.5 = (f32[256,1]{1,0:T(8,128)S(1)}, f32[256,1]{1,0:T(8,128)S(1)}, u32[]{:S(2)}, u32[]{:S(2)}) collective-permute-start(f32[256,1]{1,0:T(8,128)S(1)} %get-tuple-element.54), channel_id=1, source_target_pairs={{0,1},{2,3},{4,5},{6,7},{8,9},{10,11},{12,13},{14,15},{16,17},{18,... | collective-permute-start | bytes 3080 | tf_op jit(solution)/shard_map/ppermute | solution.py:32
  387.6 6.9 %collective-permute-start.6 = (f32[256,1]{1,0:T(8,128)S(1)}, f32[256,1]{1,0:T(8,128)S(1)}, u32[]{:S(2)}, u32[]{:S(2)}) collective-permute-start(f32[256,1]{1,0:T(8,128)S(1)} %get-tuple-element.49), channel_id=1, source_target_pairs={{1,0},{3,2},{5,4},{7,6},{9,8},{11,10},{13,12},{15,14},{17,16},{19,... | collective-permute-start | bytes 3080 | tf_op jit(solution)/shard_map/ppermute | solution.py:34
  388.9 7.1 %collective-permute-start.7 = (f32[256,1]{1,0:T(8,128)S(1)}, f32[256,1]{1,0:T(8,128)S(1)}, u32[]{:S(2)}, u32[]{:S(2)}) collective-permute-start(f32[256,1]{1,0:T(8,128)S(1)} %get-tuple-element.50), channel_id=1, source_target_pairs={{0,1},{2,3},{4,5},{6,7},{8,9},{10,11},{12,13},{14,15},{16,17},{18,... | collective-permute-start | bytes 3080 | tf_op jit(solution)/shard_map/ppermute | solution.py:32
  397.5 6.9 %collective-permute-start.8 = (f32[256,1]{1,0:T(8,128)S(1)}, f32[256,1]{1,0:T(8,128)S(1)}, u32[]{:S(2)}, u32[]{:S(2)}) collective-permute-start(f32[256,1]{1,0:T(8,128)S(1)} %get-tuple-element.45), channel_id=1, source_target_pairs={{1,0},{3,2},{5,4},{7,6},{9,8},{11,10},{13,12},{15,14},{17,16},{19,... | collective-permute-start | bytes 3080 | tf_op jit(solution)/shard_map/ppermute | solution.py:34
  398.8 7.1 %collective-permute-start.9 = (f32[256,1]{1,0:T(8,128)S(1)}, f32[256,1]{1,0:T(8,128)S(1)}, u32[]{:S(2)}, u32[]{:S(2)}) collective-permute-start(f32[256,1]{1,0:T(8,128)S(1)} %get-tuple-element.46), channel_id=1, source_target_pairs={{0,1},{2,3},{4,5},{6,7},{8,9},{10,11},{12,13},{14,15},{16,17},{18,... | collective-permute-start | bytes 3080 | tf_op jit(solution)/shard_map/ppermute | solution.py:32
  407.3 6.9 %collective-permute-start.10 = (f32[256,1]{1,0:T(8,128)S(1)}, f32[256,1]{1,0:T(8,128)S(1)}, u32[]{:S(2)}, u32[]{:S(2)}) collective-permute-start(f32[256,1]{1,0:T(8,128)S(1)} %get-tuple-element.41), channel_id=1, source_target_pairs={{1,0},{3,2},{5,4},{7,6},{9,8},{11,10},{13,12},{15,14},{17,16},{19,... | collective-permute-start | bytes 3080 | tf_op jit(solution)/shard_map/ppermute | solution.py:34
  408.6 7.1 %collective-permute-start.11 = (f32[256,1]{1,0:T(8,128)S(1)}, f32[256,1]{1,0:T(8,128)S(1)}, u32[]{:S(2)}, u32[]{:S(2)}) collective-permute-start(f32[256,1]{1,0:T(8,128)S(1)} %get-tuple-element.42), channel_id=1, source_target_pairs={{0,1},{2,3},{4,5},{6,7},{8,9},{10,11},{12,13},{14,15},{16,17},{18,... | collective-permute-start | bytes 3080 | tf_op jit(solution)/shard_map/ppermute | solution.py:32
  417.2 6.9 %collective-permute-start.12 = (f32[256,1]{1,0:T(8,128)S(1)}, f32[256,1]{1,0:T(8,128)S(1)}, u32[]{:S(2)}, u32[]{:S(2)}) collective-permute-start(f32[256,1]{1,0:T(8,128)S(1)} %get-tuple-element.37), channel_id=1, source_target_pairs={{1,0},{3,2},{5,4},{7,6},{9,8},{11,10},{13,12},{15,14},{17,16},{19,... | collective-permute-start | bytes 3080 | tf_op jit(solution)/shard_map/ppermute | solution.py:34
  418.5 7.1 %collective-permute-start.13 = (f32[256,1]{1,0:T(8,128)S(1)}, f32[256,1]{1,0:T(8,128)S(1)}, u32[]{:S(2)}, u32[]{:S(2)}) collective-permute-start(f32[256,1]{1,0:T(8,128)S(1)} %get-tuple-element.38), channel_id=1, source_target_pairs={{0,1},{2,3},{4,5},{6,7},{8,9},{10,11},{12,13},{14,15},{16,17},{18,... | collective-permute-start | bytes 3080 | tf_op jit(solution)/shard_map/ppermute | solution.py:32
  427.0 7.2 %collective-permute-start.14 = (f32[256,1]{1,0:T(8,128)S(1)}, f32[256,1]{1,0:T(8,128)S(1)}, u32[]{:S(2)}, u32[]{:S(2)}) collective-permute-start(f32[256,1]{1,0:T(8,128)S(1)} %get-tuple-element.33), channel_id=1, source_target_pairs={{1,0},{3,2},{5,4},{7,6},{9,8},{11,10},{13,12},{15,14},{17,16},{19,... | collective-permute-start | bytes 3080 | tf_op jit(solution)/shard_map/ppermute | solution.py:34
  428.3 7.7 %collective-permute-start.15 = (f32[256,1]{1,0:T(8,128)S(1)}, f32[256,1]{1,0:T(8,128)S(1)}, u32[]{:S(2)}, u32[]{:S(2)}) collective-permute-start(f32[256,1]{1,0:T(8,128)S(1)} %get-tuple-element.34), channel_id=1, source_target_pairs={{0,1},{2,3},{4,5},{6,7},{8,9},{10,11},{12,13},{14,15},{16,17},{18,... | collective-permute-start | bytes 3080 | tf_op jit(solution)/shard_map/ppermute | solution.py:32
  437.5 8.2 %collective-permute-start.16 = (f32[256,1]{1,0:T(8,128)S(1)}, f32[256,1]{1,0:T(8,128)S(1)}, u32[]{:S(2)}, u32[]{:S(2)}) collective-permute-start(f32[256,1]{1,0:T(8,128)S(1)} %get-tuple-element.29), channel_id=1, source_target_pairs={{1,0},{3,2},{5,4},{7,6},{9,8},{11,10},{13,12},{15,14},{17,16},{19,... | collective-permute-start | bytes 3080 | tf_op jit(solution)/shard_map/ppermute | solution.py:34
  438.8 8.1 %collective-permute-start.17 = (f32[256,1]{1,0:T(8,128)S(1)}, f32[256,1]{1,0:T(8,128)S(1)}, u32[]{:S(2)}, u32[]{:S(2)}) collective-permute-start(f32[256,1]{1,0:T(8,128)S(1)} %get-tuple-element.30), channel_id=1, source_target_pairs={{0,1},{2,3},{4,5},{6,7},{8,9},{10,11},{12,13},{14,15},{16,17},{18,... | collective-permute-start | bytes 3080 | tf_op jit(solution)/shard_map/ppermute | solution.py:32
  448.3 6.9 %collective-permute-start.18 = (f32[256,1]{1,0:T(8,128)S(1)}, f32[256,1]{1,0:T(8,128)S(1)}, u32[]{:S(2)}, u32[]{:S(2)}) collective-permute-start(f32[256,1]{1,0:T(8,128)S(1)} %get-tuple-element.25), channel_id=1, source_target_pairs={{1,0},{3,2},{5,4},{7,6},{9,8},{11,10},{13,12},{15,14},{17,16},{19,... | collective-permute-start | bytes 3080 | tf_op jit(solution)/shard_map/ppermute | solution.py:34
  449.6 7.1 %collective-permute-start.19 = (f32[256,1]{1,0:T(8,128)S(1)}, f32[256,1]{1,0:T(8,128)S(1)}, u32[]{:S(2)}, u32[]{:S(2)}) collective-permute-start(f32[256,1]{1,0:T(8,128)S(1)} %get-tuple-element.26), channel_id=1, source_target_pairs={{0,1},{2,3},{4,5},{6,7},{8,9},{10,11},{12,13},{14,15},{16,17},{18,... | collective-permute-start | bytes 3080 | tf_op jit(solution)/shard_map/ppermute | solution.py:32
where the time goes:
time: 464 us; the launch traced here: 460 us
  waiting for transfers between devices  217 us (47%)
  matrix products  130 us (28%)
  starting transfers between devices  57.7 us (12%)
  local copies, waits for them, and re-layouts  29.6 us (6%)
  other arithmetic  24.5 us (5%)
    ppermute x4, waiting for transfers between devices, swapped(): lax.ppermute(array, axis, [(i, i ^ 1 << stride) for i in range(lax.axis_s...  169 us
    dot_general x8, matrix products, contribute(): jnp.dot(matrix, sector_image[1], preferred_element_type=jnp.float32)  81.1 us
    ppermute x8, starting transfers between devices, extended(): lax.ppermute(tail, axis, [(i, (i + 1) % count) for i in range(ends)])  36.7 us
    all_to_all x1, waiting for transfers between devices, per_device(): lax.all_to_all(compressed, 'rng', split_axis=2, concat_axis=1, tiled=True)  25.9 us
    convert_element_type x1, local copies, waits for them, and re-layouts, per_device(): compressed = range_transform(raw_echoes, FACTOR).astype(jnp.bfloat16)  18.1 us
    dot_general x2, matrix products, complex_mix(): jnp.einsum(form, imag_in, sine_table, precision=highest)  15.6 us
    dot_general x8, matrix products, contribute(): jnp.dot(matrix, sector_image[0], preferred_element_type=jnp.float32)  12.6 us
    ppermute x8, waiting for transfers between devices, extended(): lax.ppermute(tail, axis, [(i, (i + 1) % count) for i in range(ends)])  11.9 us
  transfers between devices with their start and end apart: 21, of which 21 were waited for; matrix products, arithmetic and copies ran while one was open for 3% of the time, Pallas kernels for 0%

commit v1 on v0

v1 whole, which is shorter than its diff:
```python
import math

import jax
import jax.numpy as jnp
import numpy as np
from jax import lax
from jax.experimental import pallas as pl
from jax.experimental.pallas import tpu as pltpu
from jax.sharding import PartitionSpec as P

FACTOR = 64
ANG = 256
MERGES = 4
SWEEPS = 8

inv_root_two = 0.7071067811865476
phase_period = 8192

GROUP = 1 << MERGES
ROWS = 16
LANES = 128
diffusion_scale = math.sqrt(0.5)

VMEM_BYTES = 56 << 20


def bf16(table):
    return np.asarray(table, np.float32).astype(jnp.bfloat16)


def transform_tables(col_count, rng_count, norm_scale):
    index = np.arange(col_count)
    angle = 2.0 * np.pi / col_count * (np.outer(index, index) % col_count)
    cosine, sine = np.cos(angle) * norm_scale, np.sin(angle) * norm_scale
    real_rows = np.concatenate([cosine, sine], axis=1)
    imag_rows = np.concatenate([-sine, cosine], axis=1)
    swath = col_count // rng_count
    parts = [p[r * swath : (r + 1) * swath] for r in range(rng_count) for p in (real_rows, imag_rows)]
    twist = 2.0 * np.pi / (GROUP * col_count) * np.outer(np.arange(GROUP), index)
    return bf16(np.concatenate(parts)), np.stack([np.cos(twist), np.sin(twist)]).astype(np.float32)


def beam_table(leaf_pulses, rng_count):
    wrapped = np.outer(np.arange(ANG) - ANG // 2, np.arange(leaf_pulses)) % leaf_pulses
    angles = 2.0 * np.pi / leaf_pulses * wrapped
    norm_scale = 1.0 / math.sqrt(leaf_pulses)
    cosine, sine = np.cos(angles).T * norm_scale, np.sin(angles).T * norm_scale
    from_real = np.concatenate([cosine, -sine], axis=1)
    from_imag = np.concatenate([sine, cosine], axis=1)
    rows = leaf_pulses // rng_count
    parts = [f[r * rows : (r + 1) * rows] for r in range(rng_count) for f in (from_real, from_imag)]
    return bf16(np.concatenate(parts))


def turned(value, numerator, denominator):
    real, imag = value
    eighth = numerator * 8 % (8 * denominator) / denominator
    if eighth == 0:
        return real, imag
    if eighth == 2:
        return imag, -real
    if eighth == 1:
        return (real + imag) * inv_root_two, (imag - real) * inv_root_two
    if eighth == 3:
        return (imag - real) * inv_root_two, -(real + imag) * inv_root_two
    angle = 2.0 * math.pi * numerator / denominator
    c, s = math.cos(angle), math.sin(angle)
    return real * c + imag * s, imag * c - real * s


def small_transform(values):
    count = len(values)
    if count == 1:
        return values
    even, odd = small_transform(values[0::2]), small_transform(values[1::2])
    low, high = [], []
    for j in range(count // 2):
        real, imag = turned(odd[j], j, count)
        low.append((even[j][0] + real, even[j][1] + imag))
        high.append((even[j][0] - real, even[j][1] - imag))
    return low + high


def transform_kernel(raw_ref, matrix_ref, twist_ref, out_ref, stage_ref):
    col_count = raw_ref.shape[2] // GROUP
    pulses = raw_ref.shape[1]

    @pl.loop(0, pulses // ROWS)
    def _(step):
        rows = pl.ds(pl.multiple_of(step * ROWS, ROWS), ROWS)
        for lane in range(0, col_count, LANES):
            values = []
            for a in range(GROUP):
                cols = pl.ds(a * col_count + lane, LANES)
                values.append(tuple(raw_ref[part, rows, cols].astype(jnp.float32) for part in range(2)))
            for c, (real, imag) in enumerate(small_transform(values)):
                if c:
                    cos = twist_ref[0, c : c + 1, lane : lane + LANES]
                    sin = twist_ref[1, c : c + 1, lane : lane + LANES]
                    real, imag = real * cos + imag * sin, imag * cos - real * sin
                stage_ref[c, rows, lane : lane + LANES] = real.astype(jnp.bfloat16)
                stage_ref[c, rows, col_count + lane : col_count + lane + LANES] = imag.astype(jnp.bfloat16)

    pair = 2

    @pl.loop(0, GROUP // pair)
    def _(step):
        held = stage_ref[pl.ds(step * pair, pair)].reshape(pair * pulses, 2 * col_count)
        mixed = lax.dot_general(
            matrix_ref[...], held, (((1,), (1,)), ((), ())), preferred_element_type=jnp.float32
        ).astype(jnp.bfloat16)
        for j in range(pair):
            out_ref[step * pair + j] = mixed[:, j * pulses : (j + 1) * pulses]


def range_transform(raw_echoes, rng_count):
    pulses, samples = raw_echoes.shape[1:]
    col_count = samples // GROUP
    matrix, twist = transform_tables(col_count, rng_count, 1.0 / FACTOR)
    return pl.pallas_call(
        transform_kernel,
        out_shape=jax.ShapeDtypeStruct((GROUP, 2 * col_count, pulses), jnp.bfloat16),
        scratch_shapes=[pltpu.VMEM((GROUP, pulses, 2 * col_count), jnp.bfloat16)],
        compiler_params=pltpu.CompilerParams(vmem_limit_bytes=VMEM_BYTES),
        name="range_transform",
    )(raw_echoes, jnp.asarray(matrix), jnp.asarray(twist))


def unit_turn(steps):
    quarter = phase_period // 4
    turn = (steps + quarter // 2) // quarter
    x = (steps - turn * quarter).astype(jnp.float32) * (2.0 * math.pi / phase_period)
    x2 = x * x
    cos = 1.0 + x2 * (-1 / 2 + x2 * (1 / 24 + x2 * (-1 / 720 + x2 * (1 / 40320 + x2 * (-1 / 3628800)))))
    sin = x + x * (x2 * (-1 / 6 + x2 * (1 / 120 + x2 * (-1 / 5040 + x2 * (1 / 362880)))))
    odd = turn % 2 == 1
    cos, sin = jnp.where(odd, sin, cos), jnp.where(odd, cos, sin)
    cos = jnp.where((turn == 1) | (turn == 2), -cos, cos)
    sin = jnp.where((turn == 2) | (turn == 3), -sin, sin)
    return cos, sin


def tables_kernel(place_ref, offsets_ref, taps_ref, weights_ref, interp_ref, base_ref, step_ref):
    tap_count = taps_ref.shape[1]
    chunk = 64
    wide = taps_ref.shape[2]

    @pl.loop(0, taps_ref.shape[0])
    def _(matrix):
        for lane in range(0, wide, LANES):
            cols = slice(lane, lane + LANES)
            for a in range(0, ANG, chunk):
                index = lax.broadcasted_iota(jnp.int32, (chunk, LANES), 0) + a
                summed = jnp.zeros((chunk, LANES), jnp.float32)
                for t in range(tap_count):
                    taps = taps_ref[matrix, t : t + 1, cols]
                    summed = summed + jnp.where(taps == index, weights_ref[matrix, t : t + 1, cols], 0.0)
                interp_ref[matrix, a : a + chunk, cols] = summed.astype(jnp.bfloat16)

    first_bin = place_ref[0]
    first_leaf = place_ref[1]
    for level in range(MERGES):

        @pl.loop(0, GROUP)
        def _(leaf):
            sector = jnp.int32(0)
            for j in range(level):
                sector = sector * 2 + (leaf >> j & 1)
            offset = offsets_ref[level, first_leaf + leaf]
            where = level * GROUP + leaf
            for lane in range(0, wide, LANES):
                cols = slice(lane, lane + LANES)
                angle = sector * wide + lane + lax.broadcasted_iota(jnp.int32, (ROWS, LANES), 1)
                per_bin = offset * angle % phase_period
                bins = first_bin + GROUP * lax.broadcasted_iota(jnp.int32, (ROWS, LANES), 0)
                cos, sin = unit_turn(per_bin * bins % phase_period)
                base_ref[where, 0, :, cols] = cos * inv_root_two
                base_ref[where, 1, :, cols] = sin * inv_root_two
                cos, sin = unit_turn(per_bin[:8] * (GROUP * ROWS) % phase_period)
                step_ref[where, 0, :, cols] = cos
                step_ref[where, 1, :, cols] = sin


def merge_tables(merge_taps, merge_weights, track_offsets, place):
    level_halves = 2 * MERGES
    taps = merge_taps.reshape(level_halves, *merge_taps.shape[2:])
    weights = merge_weights.reshape(level_halves, *merge_taps.shape[2:])
    smem = pl.BlockSpec(memory_space=pltpu.SMEM)
    vmem = pl.BlockSpec(memory_space=pltpu.VMEM)
    wide = 2 * ANG
    return pl.pallas_call(
        tables_kernel,
        in_specs=[smem, smem, vmem, vmem],
        out_shape=(
            jax.ShapeDtypeStruct((level_halves, ANG, wide), jnp.bfloat16),
            jax.ShapeDtypeStruct((MERGES * GROUP, 2, ROWS, wide), jnp.float32),
            jax.ShapeDtypeStruct((MERGES * GROUP, 2, 8, wide), jnp.float32),
        ),
        compiler_params=pltpu.CompilerParams(vmem_limit_bytes=VMEM_BYTES),
        name="merge_tables",
    )(place, track_offsets, taps, weights)


def product(a, b):
    return a[0] * b[0] - a[1] * b[1], a[0] * b[1] + a[1] * b[0]


def merge_kernel(pulses_ref, beam_ref, interp_ref, base_ref, step_ref, out_ref, image_ref, mixed_ref):
    bins = pulses_ref.shape[2]
    parts = pulses_ref.shape[1]
    batch = 4

    @pl.loop(0, GROUP // batch)
    def _(step):
        leaves = pl.ds(step * batch, batch)
        held = jnp.concatenate(
            [pulses_ref[leaves, j].reshape(batch * bins, pulses_ref.shape[3]) for j in range(parts)], axis=1
        )
        formed = jnp.dot(held, beam_ref[...], preferred_element_type=jnp.float32).astype(jnp.bfloat16)
        for j in range(batch):
            rows = formed[j * bins : (j + 1) * bins]
            image_ref[step * batch + j, :bins] = rows[:, :ANG]
            image_ref[step * batch + j, bins:] = rows[:, ANG:]

    for level in range(MERGES):

        @pl.loop(0, GROUP // 2)
        def _(index):
            low = (index >> level << (level + 1)) | (index & ((1 << level) - 1))
            pair = (low, low + (1 << level))
            for side in range(2):
                mixed_ref[side] = jnp.dot(
                    image_ref[pair[side]], interp_ref[2 * level + side], preferred_element_type=jnp.float32
                )
            for lane in range(0, 2 * ANG, 2 * LANES):
                cols = slice(lane, lane + 2 * LANES)
                turns, steps = [], []
                for side in range(2):
                    where = level * GROUP + pair[side]
                    turns.append(tuple(base_ref[where, part, :, cols] for part in range(2)))
                    steps.append(
                        tuple(jnp.concatenate([step_ref[where, part, :, cols]] * (ROWS // 8)) for part in range(2))
                    )
                target = pair[lane // ANG]
                for row in range(0, bins, ROWS):
                    if row:
                        turns = [product(turns[side], steps[side]) for side in range(2)]
                    real, imag = 0.0, 0.0
                    for side in range(2):
                        held = tuple(
                            mixed_ref[side, part * bins + row : part * bins + row + ROWS, cols] for part in range(2)
                        )
                        r, i = product(turns[side], held)
                        real, imag = real + r, imag + i
                    if level == MERGES - 1:
                        out_ref[target, row : row + ROWS, :] = jnp.sqrt(real * real + imag * imag).astype(
                            out_ref.dtype
                        )
                    else:
                        image_ref[target, row : row + ROWS, :] = real.astype(jnp.bfloat16)
                        image_ref[target, bins + row : bins + row + ROWS, :] = imag.astype(jnp.bfloat16)


def merged_magnitude(pulses, beam, interp, base, step):
    bins = pulses.shape[2]
    return pl.pallas_call(
        merge_kernel,
        out_shape=jax.ShapeDtypeStruct((GROUP, bins, ANG), jnp.bfloat16),
        scratch_shapes=[
            pltpu.VMEM((GROUP, 2 * bins, ANG), jnp.bfloat16),
            pltpu.VMEM((2, 2 * bins, 2 * ANG), jnp.float32),
        ],
        compiler_params=pltpu.CompilerParams(vmem_limit_bytes=VMEM_BYTES),
        name="merged_magnitude",
    )(pulses, beam, interp, base, step)


def diffuse_kernel(ends_ref, cells_ref, below_ref, above_ref, out_ref, ping_ref, pong_ref):
    bins = cells_ref.shape[1]
    pitch = bins + 16
    first, last = ends_ref[0] == 1, ends_ref[1] == 1
    half = GROUP // 2

    blocks = [slice(h * LANES, (h + 1) * LANES) for h in range(ANG // LANES)]
    for h, cols in enumerate(blocks):
        for c in range(GROUP):
            cells = cells_ref[c, :, cols].astype(jnp.float32)
            ping_ref[h, c * pitch + 8 : c * pitch + 8 + bins] = cells * diffusion_scale
        for j in range(half):
            down, up = half + j, j
            own = ping_ref[h, (GROUP - 1 - down) * pitch + 8 : (GROUP - 1 - down) * pitch + 9]
            sent = below_ref[j : j + 1, cols].astype(jnp.float32) * diffusion_scale
            ping_ref[h, down * pitch + 7 : down * pitch + 8] = jnp.where(first, own, sent)
            own = ping_ref[h, (GROUP - 1 - up) * pitch + 7 + bins : (GROUP - 1 - up) * pitch + 8 + bins]
            sent = above_ref[j : j + 1, cols].astype(jnp.float32) * diffusion_scale
            ping_ref[h, up * pitch + 8 + bins : up * pitch + 9 + bins] = jnp.where(last, own, sent)

    def flux(upper, lower):
        difference = upper - lower
        return difference / (2.0 + difference * difference)

    sublane = lax.broadcasted_iota(jnp.int32, (8, LANES), 0)

    def tile(source, target, h, row, begin, end):
        def cells(c, shift=0):
            return source[h, pl.ds(c * pitch + row + shift, 8)]

        def before():
            near, far = pltpu.roll(cells(GROUP - 1), 1, 0), pltpu.roll(cells(GROUP - 1, -8), 1, 0)
            return jnp.where(sublane == 0, far, near)

        def after():
            near, far = pltpu.roll(cells(0), 7, 0), pltpu.roll(cells(0, 8), 7, 0)
            return jnp.where(sublane == 7, far, near)

        here = cells(begin)
        flow = flux(here, before()) if begin == 0 else None
        for c in range(begin, end):
            if c < end - 1:
                there = cells(c + 1)
            elif end == GROUP:
                there = after()
            else:
                there = None
            ahead = flux(there, here) if there is not None else None
            value = here
            if ahead is not None:
                value = value + ahead
            if flow is not None:
                value = value - flow
            target[h, pl.ds(c * pitch + row, 8)] = value
            here, flow = there, ahead

    def sweep(source, target):
        for h in range(len(blocks)):
            tile(source, target, h, 0, half, GROUP)
            tile(source, target, h, 8 + bins, 0, half)

        @pl.loop(0, bins // 8)
        def _(step):
            for h in range(len(blocks)):
                tile(source, target, h, pl.multiple_of(8 + 8 * step, 8), 0, GROUP)

    @pl.loop(0, SWEEPS // 2)
    def _(step):
        sweep(ping_ref, pong_ref)
        sweep(pong_ref, ping_ref)

    rows = LANES // GROUP

    @pl.loop(0, bins // rows)
    def _(step):
        for h, cols in enumerate(blocks):
            held = jnp.concatenate(
                [ping_ref[h, pl.ds(8 + step * rows + d, GROUP, stride=pitch)] for d in range(rows)]
            )
            out_ref[cols, pl.ds(pl.multiple_of(step * LANES, LANES), LANES)] = held.T * (1.0 / diffusion_scale)


def despeckle(cells, below, above, ends):
    bins = cells.shape[1]
    smem = pl.BlockSpec(memory_space=pltpu.SMEM)
    vmem = pl.BlockSpec(memory_space=pltpu.VMEM)
    return pl.pallas_call(
        diffuse_kernel,
        in_specs=[smem, vmem, vmem, vmem],
        out_shape=jax.ShapeDtypeStruct((ANG, GROUP * bins), jnp.float32),
        scratch_shapes=[pltpu.VMEM((ANG // LANES, GROUP * (bins + 16), LANES), jnp.float32)] * 2,
        compiler_params=pltpu.CompilerParams(vmem_limit_bytes=VMEM_BYTES),
        name="despeckle",
    )(ends, cells, below, above)


def per_device(raw_echoes, merge_taps, merge_weights, track_offsets):
    sub_count, rng_count = lax.axis_size("sub"), lax.axis_size("rng")
    leaf, position = lax.axis_index("sub"), lax.axis_index("rng")
    pulses, samples = raw_echoes.shape[1:]
    bins = samples // (GROUP * rng_count)
    groups = [[g * GROUP + i for i in range(GROUP)] for g in range(sub_count // GROUP)]
    groups = groups if len(groups) > 1 else None

    compressed = range_transform(raw_echoes, rng_count)
    place = jnp.stack([leaf % GROUP + 1 + position * (bins * GROUP), leaf // GROUP * GROUP]).astype(jnp.int32)
    tables = merge_tables(merge_taps, merge_weights, track_offsets, place)
    if groups is None:
        blocks = compressed.reshape(GROUP * rng_count, 2 * bins, pulses)
        regrouped = lax.all_to_all(blocks, ("sub", "rng"), split_axis=0, concat_axis=0, tiled=True)
    else:
        blocks = compressed.reshape(GROUP, rng_count, 2 * bins, pulses)
        blocks = lax.all_to_all(blocks, "rng", split_axis=1, concat_axis=1, tiled=True)
        regrouped = lax.all_to_all(
            blocks, "sub", split_axis=0, concat_axis=0, tiled=True, axis_index_groups=groups
        )
    regrouped = regrouped.reshape(GROUP, rng_count * 2, bins, pulses)
    beam = jnp.asarray(beam_table(pulses * rng_count, rng_count))
    magnitude = merged_magnitude(regrouped, beam, *tables)
    cells = lax.all_to_all(
        magnitude, "sub", split_axis=0, concat_axis=0, tiled=True, axis_index_groups=groups
    )
    half = GROUP // 2
    ends = rng_count - 1
    below = lax.ppermute(cells[half:, -1], "rng", [(i, i + 1) for i in range(ends)])
    above = lax.ppermute(cells[:half, 0], "rng", [(i + 1, i) for i in range(ends)])
    flags = jnp.stack([position == 0, position == rng_count - 1]).astype(jnp.int32)
    return despeckle(cells, below, above, flags)


def solution(mesh):
    in_specs = (P(None, ("sub", "rng"), None), P(), P(), P())
    out_specs = P("sub", "rng")
    return jax.shard_map(
        per_device, mesh=mesh, in_specs=in_specs, out_specs=out_specs, check_vma=False
    )
```

time: 464 us -> 133 us (0.29)
  waiting for transfers between devices: 217 us -> 57.7 us
  matrix products: 130 us -> 0 us
  Pallas kernels: 0 us -> 55.2 us
  starting transfers between devices: 57.7 us -> 15.8 us
  local copies, waits for them, and re-layouts: 29.6 us -> 1.94 us
  other arithmetic: 24.5 us -> 1.17 us
    ppermute x20 -> x2, waiting for transfers between devices: 191 us -> 3.62 us  [the longest x1 3.62 us: per_device(): lax.ppermute(cells[:half, 0], 'rng', [(i + 1, i) for i in range(ends)])]
    dot_general x28 -> x0, matrix products: 130 us -> none  [the longest x8 81.1 us: contribute(): jnp.dot(matrix, sector_image[1], preferred_element_type=jnp.float32)]
    pallas_call x0 -> x4, Pallas kernels: none -> 55.2 us  [the longest x1 20.8 us: merged_magnitude(): pl.pallas_call(merge_kernel, out_shape=jax.ShapeDtypeStruct((GROUP, bins,...]
    ppermute x20 -> x2, starting transfers between devices: 53.5 us -> 4.5 us  [the longest x1 3.21 us: per_device(): lax.ppermute(cells[half:, -1], 'rng', [(i, i + 1) for i in range(ends)])]
    all_to_all x1 -> x2, waiting for transfers between devices: 25.9 us -> 54 us  [the longest x1 31.2 us: per_device(): lax.all_to_all(blocks, ('sub', 'rng'), split_axis=0, concat_axis=0, tiled...]
    convert_element_type x1 -> x0, local copies, waits for them, and re-layouts: 18.1 us -> none  [per_device(): compressed = range_transform(raw_echoes, FACTOR).astype(jnp.bfloat16)]
    add x9 -> x0, other arithmetic: 11.5 us -> none  [the longest x8 11.5 us: diffuse(): center + diffusion_rate * (conduct(upper_diff) * upper_diff - conduct(low...]
    all_to_all x1 -> x2, starting transfers between devices: 4.26 us -> 11.3 us  [the longest x1 7.32 us: per_device(): lax.all_to_all(blocks, ('sub', 'rng'), split_axis=0, concat_axis=0, tiled...]
  transfers between devices with their start and end apart: 21 -> 4, of which waited for: 21 -> 3; matrix products, arithmetic and copies ran while one was open for 3% -> 1% of each run, Pallas kernels for 0% -> 13%
where the time goes in v1:
time: 133 us; the launch traced here: 132 us
  waiting for transfers between devices  57.7 us (43%)
  Pallas kernels  55.2 us (42%)
  starting transfers between devices  15.8 us (12%)
  local copies, waits for them, and re-layouts  1.94 us (1%)
    all_to_all x1, waiting for transfers between devices, per_device(): lax.all_to_all(blocks, ('sub', 'rng'), split_axis=0, concat_axis=0, tiled...  31.2 us
    all_to_all x1, waiting for transfers between devices, per_device(): lax.all_to_all(magnitude, 'sub', split_axis=0, concat_axis=0, tiled=True,...  22.9 us
    pallas_call x1, Pallas kernels, merged_magnitude(): pl.pallas_call(merge_kernel, out_shape=jax.ShapeDtypeStruct((GROUP, bins,...  20.8 us
    pallas_call x1, Pallas kernels, merge_tables(): pl.pallas_call(tables_kernel, in_specs=[smem, smem, vmem, vmem], out_shap...  16.9 us
    pallas_call x1, Pallas kernels, despeckle(): pl.pallas_call(diffuse_kernel, in_specs=[smem, vmem, vmem, vmem], out_sha...  10.2 us
    all_to_all x1, starting transfers between devices, per_device(): lax.all_to_all(blocks, ('sub', 'rng'), split_axis=0, concat_axis=0, tiled...  7.32 us
    pallas_call x1, Pallas kernels, range_transform(): pl.pallas_call(transform_kernel, out_shape=jax.ShapeDtypeStruct((GROUP, 2...  7.3 us
    all_to_all x1, starting transfers between devices, per_device(): lax.all_to_all(magnitude, 'sub', split_axis=0, concat_axis=0, tiled=True,...  3.95 us
  transfers between devices with their start and end apart: 4, of which 3 were waited for; matrix products, arithmetic and copies ran while one was open for 1% of the time, Pallas kernels for 13%

profile of v1, /device:TPU:0, one launch (start us, length us, event | category | flops | bytes accessed | tf_op | source)
XLA Modules:
  0.0 131.8 jit_solution(583188624818656384)
XLA Ops:
  0.0 7.3 %range_transform.1 = bf16[16,512,128]{2,1,0:T(8,128)(2,1)} custom-call(bf16[2,128,4096]{2,1,0:T(8,128)(2,1)} %raw_ref.1, bf16[512,512]{1,0:T(8,128)(2,1)} %constant.44.clone.matrix_ref, f32[2,16,256]{2,1,0:T(8,128)} %constant.45.clone.twist_ref), custom_call_target="tpu_custom_call" | custom-call | tf_op jit(solution)/shard_map/range_transform/pallas_call | solution.py:120
  7.3 7.3 %all-to-all-start = ((bf16[32,256,128]{2,1,0:T(8,128)(2,1)}), bf16[32,256,128]{2,1,0:T(8,128)(2,1)S(1)}, u32[]{:S(2)}, u32[]{:S(2)}) async-start(bf16[32,256,128]{2,1,0:T(8,128)(2,1)} %bitcast.14), calls=%async_computation | async-start | bytes 4194304 | tf_op jit(solution)/shard_map/all_to_all | solution.py:387
  14.7 0.6 pad_add_fusion.place_ref
  15.2 16.9 %merge_tables.1 = (bf16[8,256,512]{2,1,0:T(8,128)(2,1)}, f32[64,2,16,512]{3,2,1,0:T(8,128)}, f32[64,2,8,512]{3,2,1,0:T(8,128)}) custom-call(s32[2]{0:T(128)} %pad_add_fusion.place_ref, s32[4,16]{1,0:T(4,128)} %offsets_ref.1, s32[8,8,512]{2,1,0:T(8,128)} %bitcast.16, f32[8,8,512]{2,1,0:T(8,128)} %bitcast.17), custom_call_target="tpu_custom_call" | custom-call | tf_op jit(solution)/shard_map/merge_tables/pallas_call | solution.py:191
  32.1 31.2 %all-to-all-done = bf16[32,256,128]{2,1,0:T(8,128)(2,1)S(1)} async-done(((bf16[32,256,128]{2,1,0:T(8,128)(2,1)}), bf16[32,256,128]{2,1,0:T(8,128)(2,1)S(1)}, u32[]{:S(2)}, u32[]{:S(2)}) %all-to-all-start) | async-done | bytes 2097184 | tf_op jit(solution)/shard_map/all_to_all | solution.py:387
  63.3 0.0 copy-start
  63.3 1.3 copy-done
  64.6 20.8 %merged_magnitude.1 = bf16[16,128,256]{2,1,0:T(8,128)(2,1)} custom-call(bf16[16,4,128,128]{3,2,1,0:T(8,128)(2,1)} %bitcast.15, bf16[512,512]{1,0:T(8,128)(2,1)} %constant.46.clone.beam_ref, bf16[8,256,512]{2,1,0:T(8,128)(2,1)} %get-tuple-element.8.interp_ref, f32[64,2,16,512]{3,2,1,0:T(8,128)} %get-tuple-element.9.base_ref, ...), custom_call_target="tpu_custom_call" | custom-call | tf_op jit(solution)/shard_map/merged_magnitude/pallas_call | solution.py:266
  85.4 3.9 %all-to-all-start.1 = ((bf16[16,128,256]{2,1,0:T(8,128)(2,1)}), bf16[16,128,256]{2,1,0:T(8,128)(2,1)S(1)}, u32[]{:S(2)}, u32[]{:S(2)}) async-start(bf16[16,128,256]{2,1,0:T(8,128)(2,1)} %merged_magnitude.1), calls=%async_computation.1 | async-start | bytes 2097152 | tf_op jit(solution)/shard_map/all_to_all | solution.py:397
  89.4 22.9 %all-to-all-done.1.cells_ref = bf16[16,128,256]{2,1,0:T(8,128)(2,1)S(1)} async-done(((bf16[16,128,256]{2,1,0:T(8,128)(2,1)}), bf16[16,128,256]{2,1,0:T(8,128)(2,1)S(1)}, u32[]{:S(2)}, u32[]{:S(2)}) %all-to-all-start.1) | async-done | bytes 1048608 | tf_op jit(solution)/shard_map/all_to_all | solution.py:397
  112.2 0.0 copy-start.1
  112.3 3.2 %collective-permute-start = (bf16[8,256]{1,0:T(8,128)(2,1)S(1)}, bf16[8,256]{1,0:T(8,128)(2,1)S(1)}, u32[]{:S(2)}, u32[]{:S(2)}) collective-permute-start(bf16[8,256]{1,0:T(8,128)(2,1)S(1)} %bitcast.19), channel_id=1, source_target_pairs={{0,1},{2,3},{4,5},{6,7},{8,9},{10,11},{12,13},{14,15},{16,17},{18,... | collective-permute-start | bytes 12296 | tf_op jit(solution)/shard_map/ppermute | solution.py:402
  115.5 1.3 collective-permute-start.1
  116.8 0.6 add_convert_fusion.ends_ref
  117.4 0.0 collective-permute-done.below_ref
  117.4 0.0 copy-start.2
  117.4 3.6 %collective-permute-done.1.above_ref = bf16[8,256]{1,0:T(8,128)(2,1)S(1)} collective-permute-done((bf16[8,256]{1,0:T(8,128)(2,1)S(1)}, bf16[8,256]{1,0:T(8,128)(2,1)S(1)}, u32[]{:S(2)}, u32[]{:S(2)}) %collective-permute-start.1) | collective-permute-done | bytes 4128 | tf_op jit(solution)/shard_map/ppermute | solution.py:403
  121.0 0.0 copy-done.1
  121.0 0.0 copy-done.2
  121.0 0.0 copy-start.3
  121.0 0.6 copy-done.3
  121.6 10.2 %despeckle.1 = f32[256,2048]{1,0:T(8,128)} custom-call(s32[2]{0:T(128)} %add_convert_fusion.ends_ref, bf16[16,128,256]{2,1,0:T(8,128)(2,1)} %copy-done.1, bf16[8,256]{1,0:T(8,128)(2,1)} %copy-done.2, bf16[8,256]{1,0:T(8,128)(2,1)} %copy-done.3), custom_call_target="tpu_custom_call" | custom-call | tf_op jit(solution)/shard_map/despeckle/pallas_call | solution.py:364
  (3 shorter events, 0.0 us)
Async XLA Ops:
  7.3 56.0 %all-to-all-start = ((bf16[32,256,128]{2,1,0:T(8,128)(2,1)}), bf16[32,256,128]{2,1,0:T(8,128)(2,1)S(1)}, u32[]{:S(2)}, u32[]{:S(2)}) async-start(bf16[32,256,128]{2,1,0:T(8,128)(2,1)} %bitcast.14), calls=%async_computation | async-start | bytes 4194304 | tf_op jit(solution)/shard_map/all_to_all | solution.py:387
  63.3 1.3 %copy-start = (bf16[32,256,128]{2,1,0:T(8,128)(2,1)}, bf16[32,256,128]{2,1,0:T(8,128)(2,1)S(1)}, u32[]{:S(2)}) copy-start(bf16[32,256,128]{2,1,0:T(8,128)(2,1)S(1)} %all-to-all-done) | copy-start | bytes 6291460
  85.4 26.8 %all-to-all-start.1 = ((bf16[16,128,256]{2,1,0:T(8,128)(2,1)}), bf16[16,128,256]{2,1,0:T(8,128)(2,1)S(1)}, u32[]{:S(2)}, u32[]{:S(2)}) async-start(bf16[16,128,256]{2,1,0:T(8,128)(2,1)} %merged_magnitude.1), calls=%async_computation.1 | async-start | bytes 2097152 | tf_op jit(solution)/shard_map/all_to_all | solution.py:397
  112.2 8.8 %copy-start.1 = (bf16[16,128,256]{2,1,0:T(8,128)(2,1)}, bf16[16,128,256]{2,1,0:T(8,128)(2,1)S(1)}, u32[]{:S(2)}) copy-start(bf16[16,128,256]{2,1,0:T(8,128)(2,1)S(1)} %all-to-all-done.1.cells_ref) | copy-start | bytes 3145732
  112.3 5.1 %collective-permute-start = (bf16[8,256]{1,0:T(8,128)(2,1)S(1)}, bf16[8,256]{1,0:T(8,128)(2,1)S(1)}, u32[]{:S(2)}, u32[]{:S(2)}) collective-permute-start(bf16[8,256]{1,0:T(8,128)(2,1)S(1)} %bitcast.19), channel_id=1, source_target_pairs={{0,1},{2,3},{4,5},{6,7},{8,9},{10,11},{12,13},{14,15},{16,17},{18,... | collective-permute-start | bytes 12296 | tf_op jit(solution)/shard_map/ppermute | solution.py:402
  115.5 5.5 %collective-permute-start.1 = (bf16[8,256]{1,0:T(8,128)(2,1)S(1)}, bf16[8,256]{1,0:T(8,128)(2,1)S(1)}, u32[]{:S(2)}, u32[]{:S(2)}) collective-permute-start(bf16[8,256]{1,0:T(8,128)(2,1)S(1)} %bitcast.18), channel_id=1, source_target_pairs={{1,0},{3,2},{5,4},{7,6},{9,8},{11,10},{13,12},{15,14},{17,16},{19,... | collective-permute-start | bytes 12296 | tf_op jit(solution)/shard_map/ppermute | solution.py:403
  117.4 3.6 %copy-start.2 = (bf16[8,256]{1,0:T(8,128)(2,1)}, bf16[8,256]{1,0:T(8,128)(2,1)S(1)}, u32[]{:S(2)}) copy-start(bf16[8,256]{1,0:T(8,128)(2,1)S(1)} %collective-permute-done.below_ref) | copy-start | bytes 12292
  121.0 0.6 copy-start.3

commit v2 on v1

--- a/solution.py
+++ b/solution.py
@@ -1,3 +1,4 @@
+import functools
 import math
 
 import jax
@@ -23,9 +24,24 @@
 
 VMEM_BYTES = 56 << 20
 
+ANY = pl.BlockSpec(memory_space=pl.ANY)
+SMEM = pl.BlockSpec(memory_space=pltpu.SMEM)
+VMEM = pl.BlockSpec(memory_space=pltpu.VMEM)
+
 
 def bf16(table):
     return np.asarray(table, np.float32).astype(jnp.bfloat16)
+
+
+def chunked(bins):
+    quarter = bins // 4
+    if quarter % ROWS:
+        return (((0, bins),),)
+    return ((0, quarter), (3 * quarter, quarter)), ((quarter, 2 * quarter),)
+
+
+def length(segments):
+    return sum(count for _, count in segments)
 
 
 def transform_tables(col_count, rng_count, norm_scale):
@@ -35,7 +51,13 @@
     real_rows = np.concatenate([cosine, sine], axis=1)
     imag_rows = np.concatenate([-sine, cosine], axis=1)
     swath = col_count // rng_count
-    parts = [p[r * swath : (r + 1) * swath] for r in range(rng_count) for p in (real_rows, imag_rows)]
+    parts = [
+        part[r * swath + start : r * swath + start + count]
+        for segments in chunked(swath)
+        for r in range(rng_count)
+        for part in (real_rows, imag_rows)
+        for start, count in segments
+    ]
     twist = 2.0 * np.pi / (GROUP * col_count) * np.outer(np.arange(GROUP), index)
     return bf16(np.concatenate(parts)), np.stack([np.cos(twist), np.sin(twist)]).astype(np.float32)
 
@@ -81,27 +103,51 @@
     return low + high
 
 
-def transform_kernel(raw_ref, matrix_ref, twist_ref, out_ref, stage_ref):
+def transform_kernel(raw_hbm, matrix_hbm, twist_ref, *refs):
+    count = (len(refs) - 6) // 2
+    out_hbms, refs = refs[:count], refs[count:]
+    raw_ref, matrix_ref, stage_ref, *out_refs = refs[: 3 + count]
+    raw_sems, matrix_sem, out_sems = refs[3 + count :]
     col_count = raw_ref.shape[2] // GROUP
     pulses = raw_ref.shape[1]
-
-    @pl.loop(0, pulses // ROWS)
-    def _(step):
-        rows = pl.ds(pl.multiple_of(step * ROWS, ROWS), ROWS)
-        for lane in range(0, col_count, LANES):
-            values = []
-            for a in range(GROUP):
-                cols = pl.ds(a * col_count + lane, LANES)
-                values.append(tuple(raw_ref[part, rows, cols].astype(jnp.float32) for part in range(2)))
-            for c, (real, imag) in enumerate(small_transform(values)):
-                if c:
-                    cos = twist_ref[0, c : c + 1, lane : lane + LANES]
-                    sin = twist_ref[1, c : c + 1, lane : lane + LANES]
-                    real, imag = real * cos + imag * sin, imag * cos - real * sin
-                stage_ref[c, rows, lane : lane + LANES] = real.astype(jnp.bfloat16)
-                stage_ref[c, rows, col_count + lane : col_count + lane + LANES] = imag.astype(jnp.bfloat16)
-
+    blocks = raw_sems.shape[0]
+    block = pulses // blocks
     pair = 2
+
+    def fetch(i):
+        rows = pl.ds(pl.multiple_of(i * block, block), block)
+        return pltpu.make_async_copy(raw_hbm.at[:, rows], raw_ref.at[:, rows], raw_sems.at[i])
+
+    def send(k, step):
+        here = pl.ds(step * pair, pair)
+        return pltpu.make_async_copy(out_refs[k].at[here], out_hbms[k].at[here], out_sems.at[k, step])
+
+    matrix_copy = pltpu.make_async_copy(matrix_hbm, matrix_ref, matrix_sem)
+    for i in range(blocks):
+        fetch(i).start()
+    matrix_copy.start()
+
+    @pl.loop(0, blocks)
+    def _(i):
+        fetch(i).wait()
+
+        @pl.loop(0, block // ROWS)
+        def _(step):
+            rows = pl.ds(pl.multiple_of(i * block + step * ROWS, ROWS), ROWS)
+            for lane in range(0, col_count, LANES):
+                values = []
+                for a in range(GROUP):
+                    cols = pl.ds(a * col_count + lane, LANES)
+                    values.append(tuple(raw_ref[part, rows, cols].astype(jnp.float32) for part in range(2)))
+                for c, (real, imag) in enumerate(small_transform(values)):
+                    if c:
+                        cos = twist_ref[0, c : c + 1, lane : lane + LANES]
+                        sin = twist_ref[1, c : c + 1, lane : lane + LANES]
+                        real, imag = real * cos + imag * sin, imag * cos - real * sin
+                    stage_ref[c, rows, lane : lane + LANES] = real.astype(jnp.bfloat16)
+                    stage_ref[c, rows, col_count + lane : col_count + lane + LANES] = imag.astype(jnp.bfloat16)
+
+    matrix_copy.wait()
 
     @pl.loop(0, GROUP // pair)
     def _(step):
@@ -109,18 +155,38 @@
         mixed = lax.dot_general(
             matrix_ref[...], held, (((1,), (1,)), ((), ())), preferred_element_type=jnp.float32
         ).astype(jnp.bfloat16)
-        for j in range(pair):
-            out_ref[step * pair + j] = mixed[:, j * pulses : (j + 1) * pulses]
+        begin = 0
+        for k, out_ref in enumerate(out_refs):
+            end = begin + out_ref.shape[1]
+            for j in range(pair):
+                out_ref[step * pair + j] = mixed[begin:end, j * pulses : (j + 1) * pulses]
+            begin = end
+            send(k, step).start()
+
+    for k in range(count):
+        for step in range(GROUP // pair):
+            send(k, step).wait()
 
 
 def range_transform(raw_echoes, rng_count):
     pulses, samples = raw_echoes.shape[1:]
     col_count = samples // GROUP
     matrix, twist = transform_tables(col_count, rng_count, 1.0 / FACTOR)
+    outputs = [(GROUP, rng_count * 2 * length(segments), pulses) for segments in chunked(col_count // rng_count)]
     return pl.pallas_call(
         transform_kernel,
-        out_shape=jax.ShapeDtypeStruct((GROUP, 2 * col_count, pulses), jnp.bfloat16),
-        scratch_shapes=[pltpu.VMEM((GROUP, pulses, 2 * col_count), jnp.bfloat16)],
+        in_specs=[ANY, ANY, VMEM],
+        out_specs=(ANY,) * len(outputs),
+        out_shape=tuple(jax.ShapeDtypeStruct(shape, jnp.bfloat16) for shape in outputs),
+        scratch_shapes=[
+            pltpu.VMEM(raw_echoes.shape, jnp.bfloat16),
+            pltpu.VMEM(matrix.shape, jnp.bfloat16),
+            pltpu.VMEM((GROUP, pulses, 2 * col_count), jnp.bfloat16),
+            *[pltpu.VMEM(shape, jnp.bfloat16) for shape in outputs],
+            pltpu.SemaphoreType.DMA((pulses // (2 * ROWS),)),
+            pltpu.SemaphoreType.DMA,
+            pltpu.SemaphoreType.DMA((len(outputs), GROUP // 2)),
+        ],
         compiler_params=pltpu.CompilerParams(vmem_limit_bytes=VMEM_BYTES),
         name="range_transform",
     )(raw_echoes, jnp.asarray(matrix), jnp.asarray(twist))
@@ -170,31 +236,29 @@
             where = level * GROUP + leaf
             for lane in range(0, wide, LANES):
                 cols = slice(lane, lane + LANES)
-                angle = sector * wide + lane + lax.broadcasted_iota(jnp.int32, (ROWS, LANES), 1)
+                angle = sector * wide + lane + lax.broadcasted_iota(jnp.int32, (8, LANES), 1)
                 per_bin = offset * angle % phase_period
-                bins = first_bin + GROUP * lax.broadcasted_iota(jnp.int32, (ROWS, LANES), 0)
+                bins = first_bin + GROUP * lax.broadcasted_iota(jnp.int32, (8, LANES), 0)
                 cos, sin = unit_turn(per_bin * bins % phase_period)
                 base_ref[where, 0, :, cols] = cos * inv_root_two
                 base_ref[where, 1, :, cols] = sin * inv_root_two
-                cos, sin = unit_turn(per_bin[:8] * (GROUP * ROWS) % phase_period)
-                step_ref[where, 0, :, cols] = cos
-                step_ref[where, 1, :, cols] = sin
+                cos, sin = unit_turn(per_bin[:1] * (GROUP * 8) % phase_period)
+                step_ref[where, 0:1, cols] = cos
+                step_ref[where, 1:2, cols] = sin
 
 
 def merge_tables(merge_taps, merge_weights, track_offsets, place):
     level_halves = 2 * MERGES
     taps = merge_taps.reshape(level_halves, *merge_taps.shape[2:])
     weights = merge_weights.reshape(level_halves, *merge_taps.shape[2:])
-    smem = pl.BlockSpec(memory_space=pltpu.SMEM)
-    vmem = pl.BlockSpec(memory_space=pltpu.VMEM)
     wide = 2 * ANG
     return pl.pallas_call(
         tables_kernel,
-        in_specs=[smem, smem, vmem, vmem],
+        in_specs=[SMEM, SMEM, VMEM, VMEM],
         out_shape=(
             jax.ShapeDtypeStruct((level_halves, ANG, wide), jnp.bfloat16),
-            jax.ShapeDtypeStruct((MERGES * GROUP, 2, ROWS, wide), jnp.float32),
             jax.ShapeDtypeStruct((MERGES * GROUP, 2, 8, wide), jnp.float32),
+            jax.ShapeDtypeStruct((MERGES * GROUP, 2, wide), jnp.float32),
         ),
         compiler_params=pltpu.CompilerParams(vmem_limit_bytes=VMEM_BYTES),
         name="merge_tables",
@@ -205,13 +269,50 @@
     return a[0] * b[0] - a[1] * b[1], a[0] * b[1] + a[1] * b[0]
 
 
-def merge_kernel(pulses_ref, beam_ref, interp_ref, base_ref, step_ref, out_ref, image_ref, mixed_ref):
+def power(a, count):
+    if count == 1:
+        return a
+    half = power(a, count // 2)
+    whole = product(half, half)
+    return product(whole, a) if count % 2 else whole
+
+
+def merge_kernel(segments, pulses_hbm, beam_hbm, interp_hbm, base_hbm, step_hbm, out_hbm, *refs):
+    pulses_ref, beam_ref, interp_ref, base_ref, step_ref, out_ref, image_ref, mixed_ref = refs[:8]
+    pulse_sems, whole_sems, level_sems, out_sems = refs[8:]
     bins = pulses_ref.shape[2]
     parts = pulses_ref.shape[1]
     batch = 4
 
+    def copy(source, target, here, sem):
+        return pltpu.make_async_copy(source.at[here], target.at[here], sem)
+
+    def pulses_copy(i):
+        return copy(pulses_hbm, pulses_ref, pl.ds(i * batch, batch), pulse_sems.at[i])
+
+    def level_copies(level):
+        return (
+            copy(interp_hbm, interp_ref, pl.ds(2 * level, 2), level_sems.at[level, 0]),
+            copy(base_hbm, base_ref, pl.ds(level * GROUP, GROUP), level_sems.at[level, 1]),
+        )
+
+    def out_copy(leaf):
+        return copy(out_ref, out_hbm, pl.ds(leaf, 1), out_sems.at[leaf])
+
+    beam_copy = pltpu.make_async_copy(beam_hbm, beam_ref, whole_sems.at[0])
+    step_copy = pltpu.make_async_copy(step_hbm, step_ref, whole_sems.at[1])
+    beam_copy.start()
+    for i in range(GROUP // batch):
+        pulses_copy(i).start()
+    step_copy.start()
+    for level in range(MERGES):
+        for item in level_copies(level):
+            item.start()
+    beam_copy.wait()
+
     @pl.loop(0, GROUP // batch)
     def _(step):
+        pulses_copy(step).wait()
         leaves = pl.ds(step * batch, batch)
         held = jnp.concatenate(
             [pulses_ref[leaves, j].reshape(batch * bins, pulses_ref.shape[3]) for j in range(parts)], axis=1
@@ -222,33 +323,50 @@
             image_ref[step * batch + j, :bins] = rows[:, :ANG]
             image_ref[step * batch + j, bins:] = rows[:, ANG:]
 
+    step_copy.wait()
     for level in range(MERGES):
+        for item in level_copies(level):
+            item.wait()
+
+        def lower(index):
+            return (index >> level << (level + 1)) | (index & ((1 << level) - 1))
+
+        @pl.loop(0, GROUP // 2 // batch)
+        def _(step):
+            for side in range(2):
+                leaves = [lower(step * batch + j) + (side << level) for j in range(batch)]
+                held = jnp.concatenate([image_ref[leaf] for leaf in leaves])
+                mixed = jnp.dot(held, interp_ref[2 * level + side], preferred_element_type=jnp.float32)
+                for j in range(batch):
+                    mixed_ref[side, step * batch + j] = mixed[j * 2 * bins : (j + 1) * 2 * bins]
 
         @pl.loop(0, GROUP // 2)
         def _(index):
-            low = (index >> level << (level + 1)) | (index & ((1 << level) - 1))
+            low = lower(index)
             pair = (low, low + (1 << level))
-            for side in range(2):
-                mixed_ref[side] = jnp.dot(
-                    image_ref[pair[side]], interp_ref[2 * level + side], preferred_element_type=jnp.float32
-                )
             for lane in range(0, 2 * ANG, 2 * LANES):
                 cols = slice(lane, lane + 2 * LANES)
                 turns, steps = [], []
                 for side in range(2):
                     where = level * GROUP + pair[side]
-                    turns.append(tuple(base_ref[where, part, :, cols] for part in range(2)))
-                    steps.append(
-                        tuple(jnp.concatenate([step_ref[where, part, :, cols]] * (ROWS // 8)) for part in range(2))
-                    )
+                    base = tuple(base_ref[where, part, :, cols] for part in range(2))
+                    step = tuple(step_ref[where, part : part + 1, cols] for part in range(2))
+                    later = product(base, step)
+                    turns.append(tuple(jnp.concatenate([base[part], later[part]]) for part in range(2)))
+                    steps.append(product(step, step))
                 target = pair[lane // ANG]
-                for row in range(0, bins, ROWS):
-                    if row:
-                        turns = [product(turns[side], steps[side]) for side in range(2)]
+                place = 0
+                spots = [start + i for start, count in segments for i in range(0, count, ROWS)]
+                for row, spot in zip(range(0, bins, ROWS), spots):
+                    if spot != place:
+                        jumps = [power(steps[side], (spot - place) // ROWS) for side in range(2)]
+                        turns = [product(turns[side], jumps[side]) for side in range(2)]
+                        place = spot
                     real, imag = 0.0, 0.0
                     for side in range(2):
                         held = tuple(
-                            mixed_ref[side, part * bins + row : part * bins + row + ROWS, cols] for part in range(2)
+                            mixed_ref[side, index, part * bins + row : part * bins + row + ROWS, cols]
+                            for part in range(2)
                         )
                         r, i = product(turns[side], held)
                         real, imag = real + r, imag + i
@@ -259,33 +377,62 @@
                     else:
                         image_ref[target, row : row + ROWS, :] = real.astype(jnp.bfloat16)
                         image_ref[target, bins + row : bins + row + ROWS, :] = imag.astype(jnp.bfloat16)
-
-
-def merged_magnitude(pulses, beam, interp, base, step):
+            if level == MERGES - 1:
+                for leaf in pair:
+                    out_copy(leaf).start()
+
+    for leaf in range(GROUP):
+        out_copy(leaf).wait()
+
+
+def merged_magnitude(segments, pulses, beam, interp, base, step):
     bins = pulses.shape[2]
+    inputs = (pulses, beam, interp, base, step)
     return pl.pallas_call(
-        merge_kernel,
+        functools.partial(merge_kernel, segments),
+        in_specs=[ANY] * len(inputs),
+        out_specs=ANY,
         out_shape=jax.ShapeDtypeStruct((GROUP, bins, ANG), jnp.bfloat16),
         scratch_shapes=[
+            *[pltpu.VMEM(array.shape, array.dtype) for array in inputs],
+            pltpu.VMEM((GROUP, bins, ANG), jnp.bfloat16),
             pltpu.VMEM((GROUP, 2 * bins, ANG), jnp.bfloat16),
-            pltpu.VMEM((2, 2 * bins, 2 * ANG), jnp.float32),
+            pltpu.VMEM((2, GROUP // 2, 2 * bins, 2 * ANG), jnp.float32),
+            pltpu.SemaphoreType.DMA((GROUP // 4,)),
+            pltpu.SemaphoreType.DMA((2,)),
+            pltpu.SemaphoreType.DMA((MERGES, 2)),
+            pltpu.SemaphoreType.DMA((GROUP,)),
         ],
         compiler_params=pltpu.CompilerParams(vmem_limit_bytes=VMEM_BYTES),
         name="merged_magnitude",
-    )(pulses, beam, interp, base, step)
-
-
-def diffuse_kernel(ends_ref, cells_ref, below_ref, above_ref, out_ref, ping_ref, pong_ref):
-    bins = cells_ref.shape[1]
+    )(*inputs)
+
+
+def diffuse_kernel(chunks, ends_ref, below_ref, above_ref, *refs):
+    count = len(chunks)
+    cells_hbms, out_hbm, cells_refs = refs[:count], refs[count], refs[count + 1 : 2 * count + 1]
+    out_ref, ping_ref, pong_ref, cells_sems, out_sems = refs[2 * count + 1 :]
+    copies = [
+        pltpu.make_async_copy(cells_hbms[k], cells_refs[k], cells_sems.at[k]) for k in range(count)
+    ]
+    for item in copies:
+        item.start()
+    bins = sum(length(segments) for segments in chunks)
     pitch = bins + 16
     first, last = ends_ref[0] == 1, ends_ref[1] == 1
     half = GROUP // 2
 
     blocks = [slice(h * LANES, (h + 1) * LANES) for h in range(ANG // LANES)]
+    for segments, cells_ref, item in zip(chunks, cells_refs, copies):
+        item.wait()
+        for h, cols in enumerate(blocks):
+            for c in range(GROUP):
+                row = 0
+                for start, length_here in segments:
+                    cells = cells_ref[c, row : row + length_here, cols].astype(jnp.float32)
+                    ping_ref[h, pl.ds(c * pitch + 8 + start, length_here)] = cells * diffusion_scale
+                    row += length_here
     for h, cols in enumerate(blocks):
-        for c in range(GROUP):
-            cells = cells_ref[c, :, cols].astype(jnp.float32)
-            ping_ref[h, c * pitch + 8 : c * pitch + 8 + bins] = cells * diffusion_scale
         for j in range(half):
             down, up = half + j, j
             own = ping_ref[h, (GROUP - 1 - down) * pitch + 8 : (GROUP - 1 - down) * pitch + 9]
@@ -348,6 +495,10 @@
 
     rows = LANES // GROUP
 
+    def out_copy(step):
+        cols = pl.ds(pl.multiple_of(step * LANES, LANES), LANES)
+        return pltpu.make_async_copy(out_ref.at[:, cols], out_hbm.at[:, cols], out_sems.at[step])
+
     @pl.loop(0, bins // rows)
     def _(step):
         for h, cols in enumerate(blocks):
@@ -355,20 +506,30 @@
                 [ping_ref[h, pl.ds(8 + step * rows + d, GROUP, stride=pitch)] for d in range(rows)]
             )
             out_ref[cols, pl.ds(pl.multiple_of(step * LANES, LANES), LANES)] = held.T * (1.0 / diffusion_scale)
-
-
-def despeckle(cells, below, above, ends):
-    bins = cells.shape[1]
-    smem = pl.BlockSpec(memory_space=pltpu.SMEM)
-    vmem = pl.BlockSpec(memory_space=pltpu.VMEM)
+        out_copy(step).start()
+
+    for step in range(bins // rows):
+        out_copy(step).wait()
+
+
+def despeckle(chunks, cells, below, above, ends):
+    bins = sum(part.shape[1] for part in cells)
+    shape = (ANG, GROUP * bins)
     return pl.pallas_call(
-        diffuse_kernel,
-        in_specs=[smem, vmem, vmem, vmem],
-        out_shape=jax.ShapeDtypeStruct((ANG, GROUP * bins), jnp.float32),
-        scratch_shapes=[pltpu.VMEM((ANG // LANES, GROUP * (bins + 16), LANES), jnp.float32)] * 2,
+        functools.partial(diffuse_kernel, chunks),
+        in_specs=[SMEM, VMEM, VMEM] + [ANY] * len(cells),
+        out_specs=ANY,
+        out_shape=jax.ShapeDtypeStruct(shape, jnp.float32),
+        scratch_shapes=[
+            *[pltpu.VMEM(part.shape, part.dtype) for part in cells],
+            pltpu.VMEM(shape, jnp.float32),
+            *[pltpu.VMEM((ANG // LANES, GROUP * (bins + 16), LANES), jnp.float32)] * 2,
+            pltpu.SemaphoreType.DMA((len(cells),)),
+            pltpu.SemaphoreType.DMA((GROUP * bins // LANES,)),
+        ],
         compiler_params=pltpu.CompilerParams(vmem_limit_bytes=VMEM_BYTES),
         name="despeckle",
-    )(ends, cells, below, above)
+    )(ends, below, above, *cells)
 
 
 def per_device(raw_echoes, merge_taps, merge_weights, track_offsets):
@@ -379,30 +540,45 @@
     groups = [[g * GROUP + i for i in range(GROUP)] for g in range(sub_count // GROUP)]
     groups = groups if len(groups) > 1 else None
 
+    chunks = chunked(bins)
+
+    def regroup(block, count):
+        if groups is None:
+            block = block.reshape(GROUP * rng_count, 2 * count, pulses)
+            block = lax.all_to_all(block, ("sub", "rng"), split_axis=0, concat_axis=0, tiled=True)
+        else:
+            block = block.reshape(GROUP, rng_count, 2 * count, pulses)
+            block = lax.all_to_all(block, "rng", split_axis=1, concat_axis=1, tiled=True)
+            block = lax.all_to_all(
+                block, "sub", split_axis=0, concat_axis=0, tiled=True, axis_index_groups=groups
+            )
+        return block.reshape(GROUP, rng_count * 2, count, pulses)
+
     compressed = range_transform(raw_echoes, rng_count)
     place = jnp.stack([leaf % GROUP + 1 + position * (bins * GROUP), leaf // GROUP * GROUP]).astype(jnp.int32)
     tables = merge_tables(merge_taps, merge_weights, track_offsets, place)
-    if groups is None:
-        blocks = compressed.reshape(GROUP * rng_count, 2 * bins, pulses)
-        regrouped = lax.all_to_all(blocks, ("sub", "rng"), split_axis=0, concat_axis=0, tiled=True)
+    regrouped = []
+    for block, segments in zip(compressed, chunks):
+        if regrouped:
+            block, tables, regrouped[-1] = lax.optimization_barrier((block, tables, regrouped[-1]))
+        regrouped.append(regroup(block, length(segments)))
+    beam = jnp.asarray(beam_table(pulses * rng_count, rng_count))
+    cells = []
+    for segments, block in zip(chunks, regrouped):
+        magnitude = merged_magnitude(segments, block, beam, *tables)
+        cells.append(
+            lax.all_to_all(magnitude, "sub", split_axis=0, concat_axis=0, tiled=True, axis_index_groups=groups)
+        )
+    half = GROUP // 2
+    head, tail = cells[0][:half, 0], cells[0][half:, -1]
+    if rng_count == 2:
+        below = above = lax.ppermute(jnp.where(position == 0, tail, head), "rng", [(0, 1), (1, 0)])
     else:
-        blocks = compressed.reshape(GROUP, rng_count, 2 * bins, pulses)
-        blocks = lax.all_to_all(blocks, "rng", split_axis=1, concat_axis=1, tiled=True)
-        regrouped = lax.all_to_all(
-            blocks, "sub", split_axis=0, concat_axis=0, tiled=True, axis_index_groups=groups
-        )
-    regrouped = regrouped.reshape(GROUP, rng_count * 2, bins, pulses)
-    beam = jnp.asarray(beam_table(pulses * rng_count, rng_count))
-    magnitude = merged_magnitude(regrouped, beam, *tables)
-    cells = lax.all_to_all(
-        magnitude, "sub", split_axis=0, concat_axis=0, tiled=True, axis_index_groups=groups
-    )
-    half = GROUP // 2
-    ends = rng_count - 1
-    below = lax.ppermute(cells[half:, -1], "rng", [(i, i + 1) for i in range(ends)])
-    above = lax.ppermute(cells[:half, 0], "rng", [(i + 1, i) for i in range(ends)])
+        ends = rng_count - 1
+        below = lax.ppermute(tail, "rng", [(i, i + 1) for i in range(ends)])
+        above = lax.ppermute(head, "rng", [(i + 1, i) for i in range(ends)])
     flags = jnp.stack([position == 0, position == rng_count - 1]).astype(jnp.int32)
-    return despeckle(cells, below, above, flags)
+    return despeckle(chunks, cells, below, above, flags)
 
 
 def solution(mesh):

time: 133 us -> 119 us (0.89)
  waiting for transfers between devices: 57.7 us -> 40.1 us
  starting transfers between devices: 15.8 us -> 20.5 us
    all_to_all x1 -> x2, waiting for transfers between devices: 22.9 us -> 12.3 us  [per_device(): lax.all_to_all(magnitude, 'sub', split_axis=0, concat_axis=0, tiled=True,...]
    all_to_all x1 -> x2, waiting for transfers between devices: 31.2 us -> 26.3 us  [regroup(): lax.all_to_all(block, ('sub', 'rng'), split_axis=0, concat_axis=0, tiled=...]
    all_to_all x1 -> x2, starting transfers between devices: 3.95 us -> 8 us  [per_device(): lax.all_to_all(magnitude, 'sub', split_axis=0, concat_axis=0, tiled=True,...]
    all_to_all x1 -> x2, starting transfers between devices: 7.32 us -> 11 us  [regroup(): lax.all_to_all(block, ('sub', 'rng'), split_axis=0, concat_axis=0, tiled=...]
    ppermute x2 -> x1, starting transfers between devices: 4.5 us -> 1.53 us  [per_device(): lax.ppermute(jnp.where(position == 0, tail, head), 'rng', [(0, 1), (1, 0)])]
    ppermute x2 -> x1, waiting for transfers between devices: 3.62 us -> 1.54 us  [per_device(): lax.ppermute(jnp.where(position == 0, tail, head), 'rng', [(0, 1), (1, 0)])]
    pallas_call x4 -> x5, Pallas kernels: 55.2 us -> 55.2 us  [the longest x2 24.8 us: merged_magnitude(): pl.pallas_call(functools.partial(merge_kernel, segments), in_specs=[ANY]...]
  transfers between devices with their start and end apart: 4 -> 5, of which waited for: 3 -> 5; matrix products, arithmetic and copies ran while one was open for 1% -> 1% of each run, Pallas kernels for 13% -> 32%
where the time goes in v2:
time: 119 us; the launch traced here: 118 us
  Pallas kernels  55.2 us (46%)
  waiting for transfers between devices  40.1 us (34%)
  starting transfers between devices  20.5 us (17%)
  other arithmetic  1.21 us (1%)
    all_to_all x2, waiting for transfers between devices, regroup(): lax.all_to_all(block, ('sub', 'rng'), split_axis=0, concat_axis=0, tiled=...  26.3 us
    pallas_call x2, Pallas kernels, merged_magnitude(): pl.pallas_call(functools.partial(merge_kernel, segments), in_specs=[ANY]...  24.8 us
    pallas_call x1, Pallas kernels, merge_tables(): pl.pallas_call(tables_kernel, in_specs=[SMEM, SMEM, VMEM, VMEM], out_shap...  13.1 us
    all_to_all x2, waiting for transfers between devices, per_device(): lax.all_to_all(magnitude, 'sub', split_axis=0, concat_axis=0, tiled=True,...  12.3 us
    all_to_all x2, starting transfers between devices, regroup(): lax.all_to_all(block, ('sub', 'rng'), split_axis=0, concat_axis=0, tiled=...  11 us
    pallas_call x1, Pallas kernels, despeckle(): pl.pallas_call(functools.partial(diffuse_kernel, chunks), in_specs=[SMEM,...  10.3 us
    all_to_all x2, starting transfers between devices, per_device(): lax.all_to_all(magnitude, 'sub', split_axis=0, concat_axis=0, tiled=True,...  8 us
    pallas_call x1, Pallas kernels, range_transform(): pl.pallas_call(transform_kernel, in_specs=[ANY, ANY, VMEM], out_specs=(AN...  6.86 us
  transfers between devices with their start and end apart: 5, of which 5 were waited for; matrix products, arithmetic and copies ran while one was open for 1% of the time, Pallas kernels for 32%

profile of v2, /device:TPU:0, one launch (start us, length us, event | category | flops | bytes accessed | tf_op | source)
XLA Modules:
  0.0 118.0 jit_solution(18293715213549942991)
XLA Ops:
  0.0 6.9 %range_transform.1 = (bf16[16,256,128]{2,1,0:T(8,128)(2,1)}, bf16[16,256,128]{2,1,0:T(8,128)(2,1)}) custom-call(bf16[2,128,4096]{2,1,0:T(8,128)(2,1)} %raw_hbm.1, bf16[512,512]{1,0:T(8,128)(2,1)} %constant.44.clone.matrix_hbm, f32[2,16,256]{2,1,0:T(8,128)} %constant.45.clone.twist_ref), custom_call_target="tpu_custom_call" | custom-call | tf_op jit(solution)/shard_map/range_transform/pallas_call | solution.py:176
  6.9 7.3 %all-to-all-start = ((bf16[32,128,128]{2,1,0:T(8,128)(2,1)}), bf16[32,128,128]{2,1,0:T(8,128)(2,1)S(1)}, u32[]{:S(2)}, u32[]{:S(2)}) async-start(bf16[32,128,128]{2,1,0:T(8,128)(2,1)} %bitcast.15), calls=%async_computation | async-start | bytes 2097152 | tf_op jit(solution)/shard_map/all_to_all | solution.py:548
  14.2 0.6 pad_add_fusion.place_ref
  14.8 13.1 %merge_tables.1 = (bf16[8,256,512]{2,1,0:T(8,128)(2,1)}, f32[64,2,8,512]{3,2,1,0:T(8,128)}, f32[64,2,512]{2,1,0:T(2,128)}) custom-call(s32[2]{0:T(128)} %pad_add_fusion.place_ref, s32[4,16]{1,0:T(4,128)} %offsets_ref.1, s32[8,8,512]{2,1,0:T(8,128)} %bitcast.16, f32[8,8,512]{2,1,0:T(8,128)} %bitcast.17), custom_call_target="tpu_custom_call" | custom-call | tf_op jit(solution)/shard_map/merge_tables/pallas_call | solution.py:255
  28.0 12.4 %all-to-all-done = bf16[32,128,128]{2,1,0:T(8,128)(2,1)S(1)} async-done(((bf16[32,128,128]{2,1,0:T(8,128)(2,1)}), bf16[32,128,128]{2,1,0:T(8,128)(2,1)S(1)}, u32[]{:S(2)}, u32[]{:S(2)}) %all-to-all-start) | async-done | bytes 1048608 | tf_op jit(solution)/shard_map/all_to_all | solution.py:548
  40.4 0.0 copy-start
  40.4 3.6 %all-to-all-start.2 = ((bf16[32,128,128]{2,1,0:T(8,128)(2,1)}), bf16[32,128,128]{2,1,0:T(8,128)(2,1)S(1)}, u32[]{:S(2)}, u32[]{:S(2)}) async-start(bf16[32,128,128]{2,1,0:T(8,128)(2,1)} %bitcast.8), calls=%async_computation.2 | async-start | bytes 2097152 | tf_op jit(solution)/shard_map/all_to_all | solution.py:548
  44.0 0.0 copy-done
  44.1 12.4 %merged_magnitude.2 = bf16[16,64,256]{2,1,0:T(8,128)(2,1)} custom-call(bf16[16,4,64,128]{3,2,1,0:T(8,128)(2,1)} %bitcast.13, bf16[512,512]{1,0:T(8,128)(2,1)} %constant.46.clone.beam_hbm, bf16[8,256,512]{2,1,0:T(8,128)(2,1)} %get-tuple-element.21.interp_hbm, f32[64,2,8,512]{3,2,1,0:T(8,128)} %get-tuple-element.22.base_hbm, ...), custom_call_target="tpu_custom_call" | custom-call | tf_op jit(solution)/shard_map/merged_magnitude/pallas_call | solution.py:391
  56.4 13.8 %all-to-all-done.2 = bf16[32,128,128]{2,1,0:T(8,128)(2,1)S(1)} async-done(((bf16[32,128,128]{2,1,0:T(8,128)(2,1)}), bf16[32,128,128]{2,1,0:T(8,128)(2,1)S(1)}, u32[]{:S(2)}, u32[]{:S(2)}) %all-to-all-start.2) | async-done | bytes 1048608 | tf_op jit(solution)/shard_map/all_to_all | solution.py:548
  70.3 0.0 copy-start.1
  70.3 3.7 %all-to-all-start.1 = ((bf16[16,64,256]{2,1,0:T(8,128)(2,1)}), bf16[16,64,256]{2,1,0:T(8,128)(2,1)S(1)}, u32[]{:S(2)}, u32[]{:S(2)}) async-start(bf16[16,64,256]{2,1,0:T(8,128)(2,1)} %merged_magnitude.2), calls=%async_computation.1 | async-start | bytes 1048576 | tf_op jit(solution)/shard_map/all_to_all | solution.py:570
  74.0 0.0 copy-done.1
  74.0 12.5 %merged_magnitude.3 = bf16[16,64,256]{2,1,0:T(8,128)(2,1)} custom-call(bf16[16,4,64,128]{3,2,1,0:T(8,128)(2,1)} %bitcast.14, bf16[512,512]{1,0:T(8,128)(2,1)} %constant.46.clone.beam_hbm, bf16[8,256,512]{2,1,0:T(8,128)(2,1)} %get-tuple-element.21.interp_hbm, f32[64,2,8,512]{3,2,1,0:T(8,128)} %get-tuple-element.22.base_hbm, ...), custom_call_target="tpu_custom_call" | custom-call | tf_op jit(solution)/shard_map/merged_magnitude/pallas_call | solution.py:391
  86.5 1.8 %all-to-all-done.1.refs_0_ = bf16[16,64,256]{2,1,0:T(8,128)(2,1)S(1)} async-done(((bf16[16,64,256]{2,1,0:T(8,128)(2,1)}), bf16[16,64,256]{2,1,0:T(8,128)(2,1)S(1)}, u32[]{:S(2)}, u32[]{:S(2)}) %all-to-all-start.1) | async-done | bytes 524320 | tf_op jit(solution)/shard_map/all_to_all | solution.py:570
  88.3 0.0 copy-start.2
  88.3 4.3 %all-to-all-start.3 = ((bf16[16,64,256]{2,1,0:T(8,128)(2,1)}), bf16[16,64,256]{2,1,0:T(8,128)(2,1)S(1)}, u32[]{:S(2)}, u32[]{:S(2)}) async-start(bf16[16,64,256]{2,1,0:T(8,128)(2,1)} %merged_magnitude.3), calls=%async_computation.3 | async-start | bytes 1048576 | tf_op jit(solution)/shard_map/all_to_all | solution.py:570
  92.6 1.5 %collective-permute-start = (bf16[8,256]{1,0:T(8,128)(2,1)S(1)}, bf16[8,256]{1,0:T(8,128)(2,1)S(1)}, u32[]{:S(2)}, u32[]{:S(2)}) collective-permute-start(bf16[8,256]{1,0:T(8,128)(2,1)S(1)} %bitcast.18), channel_id=1, source_target_pairs={{0,1},{1,0},{2,3},{3,2},{4,5},{5,4},{6,7},{7,6},{8,9},{9,8},{10,11... | collective-permute-start | bytes 12296 | tf_op jit(solution)/shard_map/ppermute | solution.py:575
  94.1 0.6 add_convert_fusion.ends_ref
  94.7 1.5 %collective-permute-done.below_ref.above_ref = bf16[8,256]{1,0:T(8,128)(2,1)S(1)} collective-permute-done((bf16[8,256]{1,0:T(8,128)(2,1)S(1)}, bf16[8,256]{1,0:T(8,128)(2,1)S(1)}, u32[]{:S(2)}, u32[]{:S(2)}) %collective-permute-start) | collective-permute-done | bytes 4128 | tf_op jit(solution)/shard_map/ppermute | solution.py:575
  96.3 0.0 copy-start.4
  96.3 10.6 %all-to-all-done.3.refs_1_ = bf16[16,64,256]{2,1,0:T(8,128)(2,1)S(1)} async-done(((bf16[16,64,256]{2,1,0:T(8,128)(2,1)}), bf16[16,64,256]{2,1,0:T(8,128)(2,1)S(1)}, u32[]{:S(2)}, u32[]{:S(2)}) %all-to-all-start.3) | async-done | bytes 524320 | tf_op jit(solution)/shard_map/all_to_all | solution.py:570
  106.8 0.0 copy-done.2
  106.8 0.0 copy-done.4
  106.8 0.0 copy-start.3
  106.8 0.8 copy-done.3
  107.6 10.3 %despeckle.1 = f32[256,2048]{1,0:T(8,128)} custom-call(s32[2]{0:T(128)} %add_convert_fusion.ends_ref, bf16[8,256]{1,0:T(8,128)(2,1)} %copy-done.4, bf16[8,256]{1,0:T(8,128)(2,1)} %copy-done.4, bf16[16,64,256]{2,1,0:T(8,128)(2,1)} %copy-done.2, bf16[16,64,256]{2,1,0:T(8,128)(2,1)} %copy-done.3), custom_call_target="tpu_custom_call" | custom-call | tf_op jit(solution)/shard_map/despeckle/pallas_call | solution.py:518
  (2 shorter events, 0.0 us)
Async XLA Ops:
  6.9 33.5 %all-to-all-start = ((bf16[32,128,128]{2,1,0:T(8,128)(2,1)}), bf16[32,128,128]{2,1,0:T(8,128)(2,1)S(1)}, u32[]{:S(2)}, u32[]{:S(2)}) async-start(bf16[32,128,128]{2,1,0:T(8,128)(2,1)} %bitcast.15), calls=%async_computation | async-start | bytes 2097152 | tf_op jit(solution)/shard_map/all_to_all | solution.py:548
  40.4 3.6 %copy-start = (bf16[32,128,128]{2,1,0:T(8,128)(2,1)}, bf16[32,128,128]{2,1,0:T(8,128)(2,1)S(1)}, u32[]{:S(2)}) copy-start(bf16[32,128,128]{2,1,0:T(8,128)(2,1)S(1)} %all-to-all-done) | copy-start | bytes 3145732
  40.4 29.8 %all-to-all-start.2 = ((bf16[32,128,128]{2,1,0:T(8,128)(2,1)}), bf16[32,128,128]{2,1,0:T(8,128)(2,1)S(1)}, u32[]{:S(2)}, u32[]{:S(2)}) async-start(bf16[32,128,128]{2,1,0:T(8,128)(2,1)} %bitcast.8), calls=%async_computation.2 | async-start | bytes 2097152 | tf_op jit(solution)/shard_map/all_to_all | solution.py:548
  70.3 3.7 %copy-start.1 = (bf16[32,128,128]{2,1,0:T(8,128)(2,1)}, bf16[32,128,128]{2,1,0:T(8,128)(2,1)S(1)}, u32[]{:S(2)}) copy-start(bf16[32,128,128]{2,1,0:T(8,128)(2,1)S(1)} %all-to-all-done.2) | copy-start | bytes 3145732
  70.3 18.0 %all-to-all-start.1 = ((bf16[16,64,256]{2,1,0:T(8,128)(2,1)}), bf16[16,64,256]{2,1,0:T(8,128)(2,1)S(1)}, u32[]{:S(2)}, u32[]{:S(2)}) async-start(bf16[16,64,256]{2,1,0:T(8,128)(2,1)} %merged_magnitude.2), calls=%async_computation.1 | async-start | bytes 1048576 | tf_op jit(solution)/shard_map/all_to_all | solution.py:570
  88.3 18.5 %copy-start.2 = (bf16[16,64,256]{2,1,0:T(8,128)(2,1)}, bf16[16,64,256]{2,1,0:T(8,128)(2,1)S(1)}, u32[]{:S(2)}) copy-start(bf16[16,64,256]{2,1,0:T(8,128)(2,1)S(1)} %all-to-all-done.1.refs_0_) | copy-start | bytes 1572868
  88.3 18.5 %all-to-all-start.3 = ((bf16[16,64,256]{2,1,0:T(8,128)(2,1)}), bf16[16,64,256]{2,1,0:T(8,128)(2,1)S(1)}, u32[]{:S(2)}, u32[]{:S(2)}) async-start(bf16[16,64,256]{2,1,0:T(8,128)(2,1)} %merged_magnitude.3), calls=%async_computation.3 | async-start | bytes 1048576 | tf_op jit(solution)/shard_map/all_to_all | solution.py:570
  92.6 3.7 %collective-permute-start = (bf16[8,256]{1,0:T(8,128)(2,1)S(1)}, bf16[8,256]{1,0:T(8,128)(2,1)S(1)}, u32[]{:S(2)}, u32[]{:S(2)}) collective-permute-start(bf16[8,256]{1,0:T(8,128)(2,1)S(1)} %bitcast.18), channel_id=1, source_target_pairs={{0,1},{1,0},{2,3},{3,2},{4,5},{5,4},{6,7},{7,6},{8,9},{9,8},{10,11... | collective-permute-start | bytes 12296 | tf_op jit(solution)/shard_map/ppermute | solution.py:575
  96.3 10.6 %copy-start.4 = (bf16[8,256]{1,0:T(8,128)(2,1)}, bf16[8,256]{1,0:T(8,128)(2,1)S(1)}, u32[]{:S(2)}) copy-start(bf16[8,256]{1,0:T(8,128)(2,1)S(1)} %collective-permute-done.below_ref.above_ref) | copy-start | bytes 12292
  106.8 0.8 copy-start.3

commit v3 on v2

--- a/solution.py
+++ b/solution.py
@@ -1,5 +1,6 @@
 import functools
 import math
+import typing
 
 import jax
 import jax.numpy as jnp
@@ -34,17 +35,17 @@
 
 
 def chunked(bins):
-    quarter = bins // 4
-    if quarter % ROWS:
+    eighth = bins // 8
+    if eighth % ROWS:
         return (((0, bins),),)
-    return ((0, quarter), (3 * quarter, quarter)), ((quarter, 2 * quarter),)
+    return ((0, 3 * eighth), (6 * eighth, 2 * eighth)), ((3 * eighth, 3 * eighth),)
 
 
 def length(segments):
     return sum(count for _, count in segments)
 
 
-def transform_tables(col_count, rng_count, norm_scale):
+def transform_tables(segments, col_count, rng_count, norm_scale):
     index = np.arange(col_count)
     angle = 2.0 * np.pi / col_count * (np.outer(index, index) % col_count)
     cosine, sine = np.cos(angle) * norm_scale, np.sin(angle) * norm_scale
@@ -53,7 +54,6 @@
     swath = col_count // rng_count
     parts = [
         part[r * swath + start : r * swath + start + count]
-        for segments in chunked(swath)
         for r in range(rng_count)
         for part in (real_rows, imag_rows)
         for start, count in segments
@@ -103,11 +103,8 @@
     return low + high
 
 
-def transform_kernel(raw_hbm, matrix_hbm, twist_ref, *refs):
-    count = (len(refs) - 6) // 2
-    out_hbms, refs = refs[:count], refs[count:]
-    raw_ref, matrix_ref, stage_ref, *out_refs = refs[: 3 + count]
-    raw_sems, matrix_sem, out_sems = refs[3 + count :]
+def transform_kernel(raw_hbm, matrix_hbm, twist_hbm, out_hbm, *refs):
+    raw_ref, matrix_ref, twist_ref, stage_ref, out_ref, raw_sems, table_sems, out_sems = refs
     col_count = raw_ref.shape[2] // GROUP
     pulses = raw_ref.shape[1]
     blocks = raw_sems.shape[0]
@@ -118,14 +115,18 @@
         rows = pl.ds(pl.multiple_of(i * block, block), block)
         return pltpu.make_async_copy(raw_hbm.at[:, rows], raw_ref.at[:, rows], raw_sems.at[i])
 
-    def send(k, step):
+    def send(step):
         here = pl.ds(step * pair, pair)
-        return pltpu.make_async_copy(out_refs[k].at[here], out_hbms[k].at[here], out_sems.at[k, step])
-
-    matrix_copy = pltpu.make_async_copy(matrix_hbm, matrix_ref, matrix_sem)
+        return pltpu.make_async_copy(out_ref.at[here], out_hbm.at[here], out_sems.at[step])
+
+    matrix_copy = pltpu.make_async_copy(matrix_hbm, matrix_ref, table_sems.at[0])
+    twist_copy = pltpu.make_async_copy(twist_hbm, twist_ref, table_sems.at[1])
     for i in range(blocks):
         fetch(i).start()
+        if i == 0:
+            twist_copy.start()
     matrix_copy.start()
+    twist_copy.wait()
 
     @pl.loop(0, blocks)
     def _(i):
@@ -155,37 +156,33 @@
         mixed = lax.dot_general(
             matrix_ref[...], held, (((1,), (1,)), ((), ())), preferred_element_type=jnp.float32
         ).astype(jnp.bfloat16)
-        begin = 0
-        for k, out_ref in enumerate(out_refs):
-            end = begin + out_ref.shape[1]
-            for j in range(pair):
-                out_ref[step * pair + j] = mixed[begin:end, j * pulses : (j + 1) * pulses]
-            begin = end
-            send(k, step).start()
-
-    for k in range(count):
-        for step in range(GROUP // pair):
-            send(k, step).wait()
-
-
-def range_transform(raw_echoes, rng_count):
+        for j in range(pair):
+            out_ref[step * pair + j] = mixed[:, j * pulses : (j + 1) * pulses]
+        send(step).start()
+
+    for step in range(GROUP // pair):
+        send(step).wait()
+
+
+def range_transform(segments, raw_echoes, rng_count):
     pulses, samples = raw_echoes.shape[1:]
     col_count = samples // GROUP
-    matrix, twist = transform_tables(col_count, rng_count, 1.0 / FACTOR)
-    outputs = [(GROUP, rng_count * 2 * length(segments), pulses) for segments in chunked(col_count // rng_count)]
+    matrix, twist = transform_tables(segments, col_count, rng_count, 1.0 / FACTOR)
+    shape = (GROUP, rng_count * 2 * length(segments), pulses)
     return pl.pallas_call(
         transform_kernel,
-        in_specs=[ANY, ANY, VMEM],
-        out_specs=(ANY,) * len(outputs),
-        out_shape=tuple(jax.ShapeDtypeStruct(shape, jnp.bfloat16) for shape in outputs),
+        in_specs=[ANY, ANY, ANY],
+        out_specs=ANY,
+        out_shape=jax.ShapeDtypeStruct(shape, jnp.bfloat16),
         scratch_shapes=[
             pltpu.VMEM(raw_echoes.shape, jnp.bfloat16),
             pltpu.VMEM(matrix.shape, jnp.bfloat16),
+            pltpu.VMEM(twist.shape, jnp.float32),
             pltpu.VMEM((GROUP, pulses, 2 * col_count), jnp.bfloat16),
-            *[pltpu.VMEM(shape, jnp.bfloat16) for shape in outputs],
+            pltpu.VMEM(shape, jnp.bfloat16),
             pltpu.SemaphoreType.DMA((pulses // (2 * ROWS),)),
-            pltpu.SemaphoreType.DMA,
-            pltpu.SemaphoreType.DMA((len(outputs), GROUP // 2)),
+            pltpu.SemaphoreType.DMA((2,)),
+            pltpu.SemaphoreType.DMA((GROUP // 2,)),
         ],
         compiler_params=pltpu.CompilerParams(vmem_limit_bytes=VMEM_BYTES),
         name="range_transform",
@@ -408,128 +405,191 @@
     )(*inputs)
 
 
-def diffuse_kernel(chunks, ends_ref, below_ref, above_ref, *refs):
-    count = len(chunks)
-    cells_hbms, out_hbm, cells_refs = refs[:count], refs[count], refs[count + 1 : 2 * count + 1]
-    out_ref, ping_ref, pong_ref, cells_sems, out_sems = refs[2 * count + 1 :]
-    copies = [
-        pltpu.make_async_copy(cells_hbms[k], cells_refs[k], cells_sems.at[k]) for k in range(count)
-    ]
-    for item in copies:
-        item.start()
-    bins = sum(length(segments) for segments in chunks)
-    pitch = bins + 16
-    first, last = ends_ref[0] == 1, ends_ref[1] == 1
+class Zone(typing.NamedTuple):
+    pieces: tuple
+    rows: int
+    begin: int
+    count: int
+    place: int
+    below: bool
+    above: bool
+
+
+def zones_of(chunks, bins):
+    if len(chunks) == 1:
+        return (Zone(((0, 0, bins, 8),), bins, 0, bins, 0, True, True),), ()
+    (_, low), (high, top) = chunks[0]
+    early = (
+        Zone(((0, 0, low, 8),), low, 0, low - 8, 0, True, False),
+        Zone(((0, low, top, 8),), top, 8, top - 8, high + 8, False, True),
+    )
+    middle = bins - low - top
+    pieces = ((0, low - ROWS, ROWS, 0), (1, 0, middle, ROWS), (0, low, ROWS, ROWS + middle))
+    late = (Zone(pieces, middle + 16, 0, middle + 16, low - 8, False, False),)
+    return early, late
+
+
+def diffuse_kernel(zones, array_count, *refs):
+    cells_hbms, out_hbm, scratch = refs[:array_count], refs[-1 - scratch_count(zones)], refs[-scratch_count(zones) :]
+    halo_hbms = refs[array_count : array_count + 2] if any(zone.below or zone.above for zone in zones) else ()
+    position = lax.axis_index("rng")
+    first, last = position == 0, position == lax.axis_size("rng") - 1
     half = GROUP // 2
-
     blocks = [slice(h * LANES, (h + 1) * LANES) for h in range(ANG // LANES)]
-    for segments, cells_ref, item in zip(chunks, cells_refs, copies):
-        item.wait()
-        for h, cols in enumerate(blocks):
-            for c in range(GROUP):
-                row = 0
-                for start, length_here in segments:
-                    cells = cells_ref[c, row : row + length_here, cols].astype(jnp.float32)
-                    ping_ref[h, pl.ds(c * pitch + 8 + start, length_here)] = cells * diffusion_scale
-                    row += length_here
-    for h, cols in enumerate(blocks):
-        for j in range(half):
-            down, up = half + j, j
-            own = ping_ref[h, (GROUP - 1 - down) * pitch + 8 : (GROUP - 1 - down) * pitch + 9]
-            sent = below_ref[j : j + 1, cols].astype(jnp.float32) * diffusion_scale
-            ping_ref[h, down * pitch + 7 : down * pitch + 8] = jnp.where(first, own, sent)
-            own = ping_ref[h, (GROUP - 1 - up) * pitch + 7 + bins : (GROUP - 1 - up) * pitch + 8 + bins]
-            sent = above_ref[j : j + 1, cols].astype(jnp.float32) * diffusion_scale
-            ping_ref[h, up * pitch + 8 + bins : up * pitch + 9 + bins] = jnp.where(last, own, sent)
+    sublane = lax.broadcasted_iota(jnp.int32, (8, LANES), 0)
+    held_zones = []
+    if halo_hbms:
+        (below_ref, above_ref, halo_sems), scratch = scratch[:3], scratch[3:]
+        halo_copies = [
+            pltpu.make_async_copy(halo_hbms[0], below_ref, halo_sems.at[0]),
+            pltpu.make_async_copy(halo_hbms[1], above_ref, halo_sems.at[1]),
+        ]
+        for item in halo_copies:
+            item.start()
+    for zone in zones:
+        pieces, scratch = scratch[: len(zone.pieces)], scratch[len(zone.pieces) :]
+        out_ref, ping_ref, pong_ref, in_sems, out_sems = scratch[:5]
+        scratch = scratch[5:]
+        copies = [
+            pltpu.make_async_copy(cells_hbms[array].at[:, pl.ds(source, rows)], pieces[k], in_sems.at[k])
+            for k, (array, source, rows, _) in enumerate(zone.pieces)
+        ]
+        for item in copies:
+            item.start()
+        held_zones.append((zone, pieces, copies, out_ref, ping_ref, pong_ref, out_sems))
 
     def flux(upper, lower):
         difference = upper - lower
         return difference / (2.0 + difference * difference)
 
-    sublane = lax.broadcasted_iota(jnp.int32, (8, LANES), 0)
-
-    def tile(source, target, h, row, begin, end):
-        def cells(c, shift=0):
-            return source[h, pl.ds(c * pitch + row + shift, 8)]
-
-        def before():
-            near, far = pltpu.roll(cells(GROUP - 1), 1, 0), pltpu.roll(cells(GROUP - 1, -8), 1, 0)
-            return jnp.where(sublane == 0, far, near)
-
-        def after():
-            near, far = pltpu.roll(cells(0), 7, 0), pltpu.roll(cells(0, 8), 7, 0)
-            return jnp.where(sublane == 7, far, near)
-
-        here = cells(begin)
-        flow = flux(here, before()) if begin == 0 else None
-        for c in range(begin, end):
-            if c < end - 1:
-                there = cells(c + 1)
-            elif end == GROUP:
-                there = after()
-            else:
-                there = None
-            ahead = flux(there, here) if there is not None else None
-            value = here
-            if ahead is not None:
-                value = value + ahead
-            if flow is not None:
-                value = value - flow
-            target[h, pl.ds(c * pitch + row, 8)] = value
-            here, flow = there, ahead
-
-    def sweep(source, target):
-        for h in range(len(blocks)):
-            tile(source, target, h, 0, half, GROUP)
-            tile(source, target, h, 8 + bins, 0, half)
-
-        @pl.loop(0, bins // 8)
+    sends = []
+    for zone, pieces, copies, out_ref, ping_ref, pong_ref, out_sems in held_zones:
+        bins = zone.rows
+        pitch = bins + 16
+        for (_, _, rows, start), piece, item in zip(zone.pieces, pieces, copies):
+            item.wait()
+            for h, cols in enumerate(blocks):
+                for c in range(GROUP):
+                    ping_ref[h, pl.ds(c * pitch + start, rows)] = (
+                        piece[c, :, cols].astype(jnp.float32) * diffusion_scale
+                    )
+        if halo_hbms and zone is zones[0]:
+            for item in halo_copies:
+                item.wait()
+        for h, cols in enumerate(blocks):
+            for j in range(half):
+                if zone.below:
+                    down = half + j
+                    own = ping_ref[h, pl.ds((GROUP - 1 - down) * pitch + 8, 1)]
+                    sent = below_ref[j : j + 1, cols].astype(jnp.float32) * diffusion_scale
+                    ping_ref[h, pl.ds(down * pitch + 7, 1)] = jnp.where(first, own, sent)
+                if zone.above:
+                    own = ping_ref[h, pl.ds((GROUP - 1 - j) * pitch + 7 + bins, 1)]
+                    sent = above_ref[j : j + 1, cols].astype(jnp.float32) * diffusion_scale
+                    ping_ref[h, pl.ds(j * pitch + 8 + bins, 1)] = jnp.where(last, own, sent)
+
+        def tile(source, target, h, row, begin, end):
+            def cells(c, shift=0):
+                return source[h, pl.ds(c * pitch + row + shift, 8)]
+
+            def before():
+                near, far = pltpu.roll(cells(GROUP - 1), 1, 0), pltpu.roll(cells(GROUP - 1, -8), 1, 0)
+                return jnp.where(sublane == 0, far, near)
+
+            def after():
+                near, far = pltpu.roll(cells(0), 7, 0), pltpu.roll(cells(0, 8), 7, 0)
+                return jnp.where(sublane == 7, far, near)
+
+            here = cells(begin)
+            flow = flux(here, before()) if begin == 0 else None
+            for c in range(begin, end):
+                if c < end - 1:
+                    there = cells(c + 1)
+                elif end == GROUP:
+                    there = after()
+                else:
+                    there = None
+                ahead = flux(there, here) if there is not None else None
+                value = here
+                if ahead is not None:
+                    value = value + ahead
+                if flow is not None:
+                    value = value - flow
+                target[h, pl.ds(c * pitch + row, 8)] = value
+                here, flow = there, ahead
+
+        def sweep(source, target):
+            for h in range(len(blocks)):
+                tile(source, target, h, 0, half, GROUP)
+                tile(source, target, h, 8 + bins, 0, half)
+
+            @pl.loop(0, bins // 8)
+            def _(step):
+                for h in range(len(blocks)):
+                    tile(source, target, h, pl.multiple_of(8 + 8 * step, 8), 0, GROUP)
+
+        @pl.loop(0, SWEEPS // 2)
         def _(step):
-            for h in range(len(blocks)):
-                tile(source, target, h, pl.multiple_of(8 + 8 * step, 8), 0, GROUP)
-
-    @pl.loop(0, SWEEPS // 2)
-    def _(step):
-        sweep(ping_ref, pong_ref)
-        sweep(pong_ref, ping_ref)
-
-    rows = LANES // GROUP
-
-    def out_copy(step):
-        cols = pl.ds(pl.multiple_of(step * LANES, LANES), LANES)
-        return pltpu.make_async_copy(out_ref.at[:, cols], out_hbm.at[:, cols], out_sems.at[step])
-
-    @pl.loop(0, bins // rows)
-    def _(step):
-        for h, cols in enumerate(blocks):
-            held = jnp.concatenate(
-                [ping_ref[h, pl.ds(8 + step * rows + d, GROUP, stride=pitch)] for d in range(rows)]
-            )
-            out_ref[cols, pl.ds(pl.multiple_of(step * LANES, LANES), LANES)] = held.T * (1.0 / diffusion_scale)
-        out_copy(step).start()
-
-    for step in range(bins // rows):
-        out_copy(step).wait()
-
-
-def despeckle(chunks, cells, below, above, ends):
-    bins = sum(part.shape[1] for part in cells)
+            sweep(ping_ref, pong_ref)
+            sweep(pong_ref, ping_ref)
+
+        rows = LANES // GROUP
+
+        def out_copy(step, zone=zone, out_ref=out_ref, out_sems=out_sems):
+            here = pl.ds(pl.multiple_of(step * LANES, LANES), LANES)
+            there = pl.ds(pl.multiple_of(zone.place * GROUP + step * LANES, LANES), LANES)
+            return pltpu.make_async_copy(out_ref.at[:, here], out_hbm.at[:, there], out_sems.at[step])
+
+        @pl.loop(0, zone.count // rows)
+        def _(step):
+            for h, cols in enumerate(blocks):
+                held = jnp.concatenate(
+                    [
+                        ping_ref[h, pl.ds(8 + zone.begin + step * rows + d, GROUP, stride=pitch)]
+                        for d in range(rows)
+                    ]
+                )
+                here = pl.ds(pl.multiple_of(step * LANES, LANES), LANES)
+                out_ref[cols, here] = held.T * (1.0 / diffusion_scale)
+            out_copy(step).start()
+
+        sends.append((out_copy, zone.count // rows))
+
+    for out_copy, count in sends:
+        for step in range(count):
+            out_copy(step).wait()
+
+
+def scratch_count(zones):
+    halo = 3 * any(zone.below or zone.above for zone in zones)
+    return halo + sum(len(zone.pieces) + 5 for zone in zones)
+
+
+def despeckle(zones, cells, halo, bins, started=()):
     shape = (ANG, GROUP * bins)
+    scratch = []
+    if halo:
+        scratch += [pltpu.VMEM(part.shape, part.dtype) for part in halo] + [pltpu.SemaphoreType.DMA((2,))]
+    for zone in zones:
+        held = pltpu.VMEM((ANG // LANES, GROUP * (zone.rows + 16), LANES), jnp.float32)
+        scratch += [
+            *[pltpu.VMEM((GROUP, rows, ANG), cells[array].dtype) for array, _, rows, _ in zone.pieces],
+            pltpu.VMEM((ANG, GROUP * zone.count), jnp.float32),
+            held,
+            held,
+            pltpu.SemaphoreType.DMA((len(zone.pieces),)),
+            pltpu.SemaphoreType.DMA((GROUP * zone.count // LANES,)),
+        ]
     return pl.pallas_call(
-        functools.partial(diffuse_kernel, chunks),
-        in_specs=[SMEM, VMEM, VMEM] + [ANY] * len(cells),
+        functools.partial(diffuse_kernel, zones, len(cells)),
+        in_specs=[ANY] * (len(cells) + len(halo) + len(started)),
         out_specs=ANY,
         out_shape=jax.ShapeDtypeStruct(shape, jnp.float32),
-        scratch_shapes=[
-            *[pltpu.VMEM(part.shape, part.dtype) for part in cells],
-            pltpu.VMEM(shape, jnp.float32),
-            *[pltpu.VMEM((ANG // LANES, GROUP * (bins + 16), LANES), jnp.float32)] * 2,
-            pltpu.SemaphoreType.DMA((len(cells),)),
-            pltpu.SemaphoreType.DMA((GROUP * bins // LANES,)),
-        ],
-        compiler_params=pltpu.CompilerParams(vmem_limit_bytes=VMEM_BYTES),
+        scratch_shapes=scratch,
+        input_output_aliases={len(cells): 0} if started else {},
+        compiler_params=pltpu.CompilerParams(vmem_limit_bytes=14 << 20),
         name="despeckle",
-    )(ends, below, above, *cells)
+    )(*cells, *halo, *started)
 
 
 def per_device(raw_echoes, merge_taps, merge_weights, track_offsets):
@@ -554,7 +614,11 @@
             )
         return block.reshape(GROUP, rng_count * 2, count, pulses)
 
-    compressed = range_transform(raw_echoes, rng_count)
+    compressed = []
+    for segments in chunks:
+        if compressed:
+            raw_echoes, compressed[-1] = lax.optimization_barrier((raw_echoes, compressed[-1]))
+        compressed.append(range_transform(segments, raw_echoes, rng_count))
     place = jnp.stack([leaf % GROUP + 1 + position * (bins * GROUP), leaf // GROUP * GROUP]).astype(jnp.int32)
     tables = merge_tables(merge_taps, merge_weights, track_offsets, place)
     regrouped = []
@@ -577,8 +641,11 @@
         ends = rng_count - 1
         below = lax.ppermute(tail, "rng", [(i, i + 1) for i in range(ends)])
         above = lax.ppermute(head, "rng", [(i + 1, i) for i in range(ends)])
-    flags = jnp.stack([position == 0, position == rng_count - 1]).astype(jnp.int32)
-    return despeckle(chunks, cells, below, above, flags)
+    early, late = zones_of(chunks, bins)
+    result = despeckle(early, cells[:1], (below, above), bins)
+    if late:
+        result = despeckle(late, cells, (), bins, (result,))
+    return result
 
 
 def solution(mesh):

time: 119 us -> 112 us (0.941)
  waiting for transfers between devices: 40.1 us -> 29.5 us
  Pallas kernels: 55.2 us -> 60.1 us
    all_to_all x2, waiting for transfers between devices: 26.3 us -> 19.3 us  [regroup(): lax.all_to_all(block, ('sub', 'rng'), split_axis=0, concat_axis=0, tiled=...]
    pallas_call x2 -> x4, Pallas kernels: 17.2 us -> 22.1 us  [the longest x2 11.1 us: range_transform(): pl.pallas_call(transform_kernel, in_specs=[ANY, ANY, ANY], out_specs=ANY,...]
    all_to_all x2, waiting for transfers between devices: 12.3 us -> 8.02 us  [per_device(): lax.all_to_all(magnitude, 'sub', split_axis=0, concat_axis=0, tiled=True,...]
  transfers between devices with their start and end apart: 5 -> 5, of which waited for: 5 -> 5; matrix products, arithmetic and copies ran while one was open for 1% -> 1% of each run, Pallas kernels for 32% -> 44%
where the time goes in v3:
time: 112 us; the launch traced here: 111 us
  Pallas kernels  60.1 us (54%)
  waiting for transfers between devices  29.5 us (26%)
  starting transfers between devices  20.9 us (19%)
    pallas_call x2, Pallas kernels, merged_magnitude(): pl.pallas_call(functools.partial(merge_kernel, segments), in_specs=[ANY]...  24.8 us
    all_to_all x2, waiting for transfers between devices, regroup(): lax.all_to_all(block, ('sub', 'rng'), split_axis=0, concat_axis=0, tiled=...  19.3 us
    pallas_call x1, Pallas kernels, merge_tables(): pl.pallas_call(tables_kernel, in_specs=[SMEM, SMEM, VMEM, VMEM], out_shap...  13.1 us
    pallas_call x2, Pallas kernels, range_transform(): pl.pallas_call(transform_kernel, in_specs=[ANY, ANY, ANY], out_specs=ANY,...  11.1 us
    pallas_call x2, Pallas kernels, despeckle(): pl.pallas_call(functools.partial(diffuse_kernel, zones, len(cells)), in_s...  11.1 us
    all_to_all x2, starting transfers between devices, regroup(): lax.all_to_all(block, ('sub', 'rng'), split_axis=0, concat_axis=0, tiled=...  11 us
    all_to_all x2, starting transfers between devices, per_device(): lax.all_to_all(magnitude, 'sub', split_axis=0, concat_axis=0, tiled=True,...  8.48 us
    all_to_all x2, waiting for transfers between devices, per_device(): lax.all_to_all(magnitude, 'sub', split_axis=0, concat_axis=0, tiled=True,...  8.02 us
  transfers between devices with their start and end apart: 5, of which 5 were waited for; matrix products, arithmetic and copies ran while one was open for 1% of the time, Pallas kernels for 44%

profile of v3, /device:TPU:0, one launch (start us, length us, event | category | flops | bytes accessed | tf_op | source)
XLA Modules:
  0.0 111.3 jit_solution(8176357432311405404)
XLA Ops:
  0.0 5.7 %range_transform.2 = bf16[16,320,128]{2,1,0:T(8,128)(2,1)} custom-call(bf16[2,128,4096]{2,1,0:T(8,128)(2,1)} %raw_hbm.2, bf16[320,512]{1,0:T(8,128)(2,1)} %constant.46.clone.matrix_hbm, f32[2,16,256]{2,1,0:T(8,128)} %constant.47.clone.twist_hbm), custom_call_target="tpu_custom_call" | custom-call | tf_op jit(solution)/shard_map/range_transform/pallas_call | solution.py:172
  5.7 7.3 %all-to-all-start = ((bf16[32,160,128]{2,1,0:T(8,128)(2,1)}), bf16[32,160,128]{2,1,0:T(8,128)(2,1)S(1)}, u32[]{:S(2)}, u32[]{:S(2)}) async-start(bf16[32,160,128]{2,1,0:T(8,128)(2,1)} %bitcast.11), calls=%async_computation | async-start | bytes 2621440 | tf_op jit(solution)/shard_map/all_to_all | solution.py:608
  13.1 5.4 %range_transform.3 = bf16[16,192,128]{2,1,0:T(8,128)(2,1)} custom-call(bf16[2,128,4096]{2,1,0:T(8,128)(2,1)} %raw_hbm.2, bf16[192,512]{1,0:T(8,128)(2,1)} %constant.48.clone.matrix_hbm, f32[2,16,256]{2,1,0:T(8,128)} %constant.47.clone.twist_hbm), custom_call_target="tpu_custom_call" | custom-call | tf_op jit(solution)/shard_map/range_transform/pallas_call | solution.py:172
  18.5 0.6 pad_add_fusion.place_ref
  19.1 13.1 %merge_tables.1 = (bf16[8,256,512]{2,1,0:T(8,128)(2,1)}, f32[64,2,8,512]{3,2,1,0:T(8,128)}, f32[64,2,512]{2,1,0:T(2,128)}) custom-call(s32[2]{0:T(128)} %pad_add_fusion.place_ref, s32[4,16]{1,0:T(4,128)} %offsets_ref.1, s32[8,8,512]{2,1,0:T(8,128)} %bitcast.15, f32[8,8,512]{2,1,0:T(8,128)} %bitcast.16), custom_call_target="tpu_custom_call" | custom-call | tf_op jit(solution)/shard_map/merge_tables/pallas_call | solution.py:252
  32.2 12.7 %all-to-all-done = bf16[32,160,128]{2,1,0:T(8,128)(2,1)S(1)} async-done(((bf16[32,160,128]{2,1,0:T(8,128)(2,1)}), bf16[32,160,128]{2,1,0:T(8,128)(2,1)S(1)}, u32[]{:S(2)}, u32[]{:S(2)}) %all-to-all-start) | async-done | bytes 1310752 | tf_op jit(solution)/shard_map/all_to_all | solution.py:608
  44.9 0.0 copy-start
  44.9 3.6 %all-to-all-start.2 = ((bf16[32,96,128]{2,1,0:T(8,128)(2,1)}), bf16[32,96,128]{2,1,0:T(8,128)(2,1)S(1)}, u32[]{:S(2)}, u32[]{:S(2)}) async-start(bf16[32,96,128]{2,1,0:T(8,128)(2,1)} %bitcast.14), calls=%async_computation.2 | async-start | bytes 1572864 | tf_op jit(solution)/shard_map/all_to_all | solution.py:608
  48.5 0.0 copy-done
  48.5 14.0 %merged_magnitude.2 = bf16[16,80,256]{2,1,0:T(8,128)(2,1)} custom-call(bf16[16,4,80,128]{3,2,1,0:T(8,128)(2,1)} %bitcast.12, bf16[512,512]{1,0:T(8,128)(2,1)} %constant.49.clone.beam_hbm, bf16[8,256,512]{2,1,0:T(8,128)(2,1)} %get-tuple-element.21.interp_hbm, f32[64,2,8,512]{3,2,1,0:T(8,128)} %get-tuple-element.22.base_hbm, ...), custom_call_target="tpu_custom_call" | custom-call | tf_op jit(solution)/shard_map/merged_magnitude/pallas_call | solution.py:388
  62.5 6.6 %all-to-all-done.2 = bf16[32,96,128]{2,1,0:T(8,128)(2,1)S(1)} async-done(((bf16[32,96,128]{2,1,0:T(8,128)(2,1)}), bf16[32,96,128]{2,1,0:T(8,128)(2,1)S(1)}, u32[]{:S(2)}, u32[]{:S(2)}) %all-to-all-start.2) | async-done | bytes 786464 | tf_op jit(solution)/shard_map/all_to_all | solution.py:608
  69.1 0.0 copy-start.1
  69.1 3.8 %all-to-all-start.1 = ((bf16[16,80,256]{2,1,0:T(8,128)(2,1)}), bf16[16,80,256]{2,1,0:T(8,128)(2,1)S(1)}, u32[]{:S(2)}, u32[]{:S(2)}) async-start(bf16[16,80,256]{2,1,0:T(8,128)(2,1)} %merged_magnitude.2), calls=%async_computation.1 | async-start | bytes 1310720 | tf_op jit(solution)/shard_map/all_to_all | solution.py:634
  72.9 0.0 copy-done.1
  72.9 10.9 %merged_magnitude.3 = bf16[16,48,256]{2,1,0:T(8,128)(2,1)} custom-call(bf16[16,4,48,128]{3,2,1,0:T(8,128)(2,1)} %bitcast.13, bf16[512,512]{1,0:T(8,128)(2,1)} %constant.49.clone.beam_hbm, bf16[8,256,512]{2,1,0:T(8,128)(2,1)} %get-tuple-element.21.interp_hbm, f32[64,2,8,512]{3,2,1,0:T(8,128)} %get-tuple-element.22.base_hbm, ...), custom_call_target="tpu_custom_call" | custom-call | tf_op jit(solution)/shard_map/merged_magnitude/pallas_call | solution.py:388
  83.8 5.7 %all-to-all-done.1.refs_0_ = bf16[16,80,256]{2,1,0:T(8,128)(2,1)S(1)} async-done(((bf16[16,80,256]{2,1,0:T(8,128)(2,1)}), bf16[16,80,256]{2,1,0:T(8,128)(2,1)S(1)}, u32[]{:S(2)}, u32[]{:S(2)}) %all-to-all-start.1) | async-done | bytes 655392 | tf_op jit(solution)/shard_map/all_to_all | solution.py:634
  89.5 4.7 %all-to-all-start.3 = ((bf16[16,48,256]{2,1,0:T(8,128)(2,1)}), bf16[16,48,256]{2,1,0:T(8,128)(2,1)S(1)}, u32[]{:S(2)}, u32[]{:S(2)}) async-start(bf16[16,48,256]{2,1,0:T(8,128)(2,1)} %merged_magnitude.3), calls=%async_computation.3 | async-start | bytes 786432 | tf_op jit(solution)/shard_map/all_to_all | solution.py:634
  94.2 1.5 %collective-permute-start = (bf16[8,256]{1,0:T(8,128)(2,1)S(1)}, bf16[8,256]{1,0:T(8,128)(2,1)S(1)}, u32[]{:S(2)}, u32[]{:S(2)}) collective-permute-start(bf16[8,256]{1,0:T(8,128)(2,1)S(1)} %bitcast.17), channel_id=1, source_target_pairs={{0,1},{1,0},{2,3},{3,2},{4,5},{5,4},{6,7},{7,6},{8,9},{9,8},{10,11... | collective-permute-start | bytes 12296 | tf_op jit(solution)/shard_map/ppermute | solution.py:639
  95.7 2.2 %collective-permute-done.refs_1_.refs_2_ = bf16[8,256]{1,0:T(8,128)(2,1)S(1)} collective-permute-done((bf16[8,256]{1,0:T(8,128)(2,1)S(1)}, bf16[8,256]{1,0:T(8,128)(2,1)S(1)}, u32[]{:S(2)}, u32[]{:S(2)}) %collective-permute-start) | collective-permute-done | bytes 4128 | tf_op jit(solution)/shard_map/ppermute | solution.py:639
  97.9 6.1 %despeckle.2.refs_2_ = f32[256,2048]{1,0:T(8,128)} custom-call(bf16[16,80,256]{2,1,0:T(8,128)(2,1)S(1)} %all-to-all-done.1.refs_0_, bf16[8,256]{1,0:T(8,128)(2,1)S(1)} %collective-permute-done.refs_1_.refs_2_, bf16[8,256]{1,0:T(8,128)(2,1)S(1)} %collective-permute-done.refs_1_.refs_2_), custom_call_target="tpu_custom_call" | custom-call | tf_op jit(solution)/shard_map/despeckle/pallas_call | solution.py:583
  104.0 2.3 %all-to-all-done.3.refs_1_ = bf16[16,48,256]{2,1,0:T(8,128)(2,1)S(1)} async-done(((bf16[16,48,256]{2,1,0:T(8,128)(2,1)}), bf16[16,48,256]{2,1,0:T(8,128)(2,1)S(1)}, u32[]{:S(2)}, u32[]{:S(2)}) %all-to-all-start.3) | async-done | bytes 393248 | tf_op jit(solution)/shard_map/all_to_all | solution.py:634
  106.3 5.0 %despeckle.3 = f32[256,2048]{1,0:T(8,128)} custom-call(bf16[16,80,256]{2,1,0:T(8,128)(2,1)S(1)} %all-to-all-done.1.refs_0_, bf16[16,48,256]{2,1,0:T(8,128)(2,1)S(1)} %all-to-all-done.3.refs_1_, f32[256,2048]{1,0:T(8,128)} %despeckle.2.refs_2_), custom_call_target="tpu_custom_call", output_to_operand_aliasing={{}: (2, {})} | custom-call | tf_op jit(solution)/shard_map/despeckle/pallas_call | solution.py:583
  (2 shorter events, 0.0 us)
Async XLA Ops:
  5.7 39.2 %all-to-all-start = ((bf16[32,160,128]{2,1,0:T(8,128)(2,1)}), bf16[32,160,128]{2,1,0:T(8,128)(2,1)S(1)}, u32[]{:S(2)}, u32[]{:S(2)}) async-start(bf16[32,160,128]{2,1,0:T(8,128)(2,1)} %bitcast.11), calls=%async_computation | async-start | bytes 2621440 | tf_op jit(solution)/shard_map/all_to_all | solution.py:608
  44.9 3.6 %copy-start = (bf16[32,160,128]{2,1,0:T(8,128)(2,1)}, bf16[32,160,128]{2,1,0:T(8,128)(2,1)S(1)}, u32[]{:S(2)}) copy-start(bf16[32,160,128]{2,1,0:T(8,128)(2,1)S(1)} %all-to-all-done) | copy-start | bytes 3932164
  44.9 24.2 %all-to-all-start.2 = ((bf16[32,96,128]{2,1,0:T(8,128)(2,1)}), bf16[32,96,128]{2,1,0:T(8,128)(2,1)S(1)}, u32[]{:S(2)}, u32[]{:S(2)}) async-start(bf16[32,96,128]{2,1,0:T(8,128)(2,1)} %bitcast.14), calls=%async_computation.2 | async-start | bytes 1572864 | tf_op jit(solution)/shard_map/all_to_all | solution.py:608
  69.1 3.8 %copy-start.1 = (bf16[32,96,128]{2,1,0:T(8,128)(2,1)}, bf16[32,96,128]{2,1,0:T(8,128)(2,1)S(1)}, u32[]{:S(2)}) copy-start(bf16[32,96,128]{2,1,0:T(8,128)(2,1)S(1)} %all-to-all-done.2) | copy-start | bytes 2359300
  69.1 20.4 %all-to-all-start.1 = ((bf16[16,80,256]{2,1,0:T(8,128)(2,1)}), bf16[16,80,256]{2,1,0:T(8,128)(2,1)S(1)}, u32[]{:S(2)}, u32[]{:S(2)}) async-start(bf16[16,80,256]{2,1,0:T(8,128)(2,1)} %merged_magnitude.2), calls=%async_computation.1 | async-start | bytes 1310720 | tf_op jit(solution)/shard_map/all_to_all | solution.py:634
  89.5 16.8 %all-to-all-start.3 = ((bf16[16,48,256]{2,1,0:T(8,128)(2,1)}), bf16[16,48,256]{2,1,0:T(8,128)(2,1)S(1)}, u32[]{:S(2)}, u32[]{:S(2)}) async-start(bf16[16,48,256]{2,1,0:T(8,128)(2,1)} %merged_magnitude.3), calls=%async_computation.3 | async-start | bytes 786432 | tf_op jit(solution)/shard_map/all_to_all | solution.py:634
  94.2 3.7 %collective-permute-start = (bf16[8,256]{1,0:T(8,128)(2,1)S(1)}, bf16[8,256]{1,0:T(8,128)(2,1)S(1)}, u32[]{:S(2)}, u32[]{:S(2)}) collective-permute-start(bf16[8,256]{1,0:T(8,128)(2,1)S(1)} %bitcast.17), channel_id=1, source_target_pairs={{0,1},{1,0},{2,3},{3,2},{4,5},{5,4},{6,7},{7,6},{8,9},{9,8},{10,11... | collective-permute-start | bytes 12296 | tf_op jit(solution)/shard_map/ppermute | solution.py:639

commit v4 on v3

--- a/solution.py
+++ b/solution.py
@@ -430,52 +430,33 @@
 
 
 def diffuse_kernel(zones, array_count, *refs):
-    cells_hbms, out_hbm, scratch = refs[:array_count], refs[-1 - scratch_count(zones)], refs[-scratch_count(zones) :]
-    halo_hbms = refs[array_count : array_count + 2] if any(zone.below or zone.above for zone in zones) else ()
+    cells_refs, out_hbm, scratch = refs[:array_count], refs[-1 - 4 * len(zones)], refs[-4 * len(zones) :]
+    halo_refs = refs[array_count : array_count + 2] if any(zone.below or zone.above for zone in zones) else ()
     position = lax.axis_index("rng")
     first, last = position == 0, position == lax.axis_size("rng") - 1
     half = GROUP // 2
     blocks = [slice(h * LANES, (h + 1) * LANES) for h in range(ANG // LANES)]
     sublane = lax.broadcasted_iota(jnp.int32, (8, LANES), 0)
+    if halo_refs:
+        below_ref, above_ref = halo_refs
     held_zones = []
-    if halo_hbms:
-        (below_ref, above_ref, halo_sems), scratch = scratch[:3], scratch[3:]
-        halo_copies = [
-            pltpu.make_async_copy(halo_hbms[0], below_ref, halo_sems.at[0]),
-            pltpu.make_async_copy(halo_hbms[1], above_ref, halo_sems.at[1]),
-        ]
-        for item in halo_copies:
-            item.start()
-    for zone in zones:
-        pieces, scratch = scratch[: len(zone.pieces)], scratch[len(zone.pieces) :]
-        out_ref, ping_ref, pong_ref, in_sems, out_sems = scratch[:5]
-        scratch = scratch[5:]
-        copies = [
-            pltpu.make_async_copy(cells_hbms[array].at[:, pl.ds(source, rows)], pieces[k], in_sems.at[k])
-            for k, (array, source, rows, _) in enumerate(zone.pieces)
-        ]
-        for item in copies:
-            item.start()
-        held_zones.append((zone, pieces, copies, out_ref, ping_ref, pong_ref, out_sems))
+    for k, zone in enumerate(zones):
+        held_zones.append((zone, *scratch[4 * k : 4 * k + 4]))
 
     def flux(upper, lower):
         difference = upper - lower
         return difference / (2.0 + difference * difference)
 
     sends = []
-    for zone, pieces, copies, out_ref, ping_ref, pong_ref, out_sems in held_zones:
+    for zone, out_ref, ping_ref, pong_ref, out_sems in held_zones:
         bins = zone.rows
         pitch = bins + 16
-        for (_, _, rows, start), piece, item in zip(zone.pieces, pieces, copies):
-            item.wait()
+        for array, source, rows, start in zone.pieces:
             for h, cols in enumerate(blocks):
                 for c in range(GROUP):
                     ping_ref[h, pl.ds(c * pitch + start, rows)] = (
-                        piece[c, :, cols].astype(jnp.float32) * diffusion_scale
+                        cells_refs[array][c, source : source + rows, cols].astype(jnp.float32) * diffusion_scale
                     )
-        if halo_hbms and zone is zones[0]:
-            for item in halo_copies:
-                item.wait()
         for h, cols in enumerate(blocks):
             for j in range(half):
                 if zone.below:
@@ -520,8 +501,10 @@
 
         def sweep(source, target):
             for h in range(len(blocks)):
-                tile(source, target, h, 0, half, GROUP)
-                tile(source, target, h, 8 + bins, 0, half)
+                if zone.below or zone.begin == 0:
+                    tile(source, target, h, 0, half, GROUP)
+                if zone.above or zone.begin + zone.count == bins:
+                    tile(source, target, h, 8 + bins, 0, half)
 
             @pl.loop(0, bins // 8)
             def _(step):
@@ -560,29 +543,20 @@
             out_copy(step).wait()
 
 
-def scratch_count(zones):
-    halo = 3 * any(zone.below or zone.above for zone in zones)
-    return halo + sum(len(zone.pieces) + 5 for zone in zones)
-
-
 def despeckle(zones, cells, halo, bins, started=()):
     shape = (ANG, GROUP * bins)
     scratch = []
-    if halo:
-        scratch += [pltpu.VMEM(part.shape, part.dtype) for part in halo] + [pltpu.SemaphoreType.DMA((2,))]
     for zone in zones:
         held = pltpu.VMEM((ANG // LANES, GROUP * (zone.rows + 16), LANES), jnp.float32)
         scratch += [
-            *[pltpu.VMEM((GROUP, rows, ANG), cells[array].dtype) for array, _, rows, _ in zone.pieces],
             pltpu.VMEM((ANG, GROUP * zone.count), jnp.float32),
             held,
             held,
-            pltpu.SemaphoreType.DMA((len(zone.pieces),)),
             pltpu.SemaphoreType.DMA((GROUP * zone.count // LANES,)),
         ]
     return pl.pallas_call(
         functools.partial(diffuse_kernel, zones, len(cells)),
-        in_specs=[ANY] * (len(cells) + len(halo) + len(started)),
+        in_specs=[VMEM] * (len(cells) + len(halo)) + [ANY] * len(started),
         out_specs=ANY,
         out_shape=jax.ShapeDtypeStruct(shape, jnp.float32),
         scratch_shapes=scratch,

time: 112 us -> 112 us (level)
  no operation moved by 1% of the time
where the time goes in v4:
time: 112 us; the launch traced here: 111 us
  Pallas kernels  59.5 us (53%)
  waiting for transfers between devices  29.9 us (27%)
  starting transfers between devices  20.9 us (19%)
    pallas_call x2, Pallas kernels, merged_magnitude(): pl.pallas_call(functools.partial(merge_kernel, segments), in_specs=[ANY]...  24.8 us
    all_to_all x2, waiting for transfers between devices, regroup(): lax.all_to_all(block, ('sub', 'rng'), split_axis=0, concat_axis=0, tiled=...  19.3 us
    pallas_call x1, Pallas kernels, merge_tables(): pl.pallas_call(tables_kernel, in_specs=[SMEM, SMEM, VMEM, VMEM], out_shap...  13.1 us
    pallas_call x2, Pallas kernels, range_transform(): pl.pallas_call(transform_kernel, in_specs=[ANY, ANY, ANY], out_specs=ANY,...  11.1 us
    all_to_all x2, starting transfers between devices, regroup(): lax.all_to_all(block, ('sub', 'rng'), split_axis=0, concat_axis=0, tiled=...  11 us
    pallas_call x2, Pallas kernels, despeckle(): pl.pallas_call(functools.partial(diffuse_kernel, zones, len(cells)), in_s...  10.5 us
    all_to_all x2, starting transfers between devices, per_device(): lax.all_to_all(magnitude, 'sub', split_axis=0, concat_axis=0, tiled=True,...  8.48 us
    all_to_all x2, waiting for transfers between devices, per_device(): lax.all_to_all(magnitude, 'sub', split_axis=0, concat_axis=0, tiled=True,...  8.37 us
  transfers between devices with their start and end apart: 5, of which 5 were waited for; matrix products, arithmetic and copies ran while one was open for 1% of the time, Pallas kernels for 44%

profile of v4, /device:TPU:0, one launch (start us, length us, event | category | flops | bytes accessed | tf_op | source)
XLA Modules:
  0.0 111.0 jit_solution(13493340583897731001)
XLA Ops:
  0.0 5.7 %range_transform.2 = bf16[16,320,128]{2,1,0:T(8,128)(2,1)} custom-call(bf16[2,128,4096]{2,1,0:T(8,128)(2,1)} %raw_hbm.2, bf16[320,512]{1,0:T(8,128)(2,1)} %constant.46.clone.matrix_hbm, f32[2,16,256]{2,1,0:T(8,128)} %constant.47.clone.twist_hbm), custom_call_target="tpu_custom_call" | custom-call | tf_op jit(solution)/shard_map/range_transform/pallas_call | solution.py:172
  5.7 7.3 %all-to-all-start = ((bf16[32,160,128]{2,1,0:T(8,128)(2,1)}), bf16[32,160,128]{2,1,0:T(8,128)(2,1)S(1)}, u32[]{:S(2)}, u32[]{:S(2)}) async-start(bf16[32,160,128]{2,1,0:T(8,128)(2,1)} %bitcast.11), calls=%async_computation | async-start | bytes 2621440 | tf_op jit(solution)/shard_map/all_to_all | solution.py:582
  13.1 5.4 %range_transform.3 = bf16[16,192,128]{2,1,0:T(8,128)(2,1)} custom-call(bf16[2,128,4096]{2,1,0:T(8,128)(2,1)} %raw_hbm.2, bf16[192,512]{1,0:T(8,128)(2,1)} %constant.48.clone.matrix_hbm, f32[2,16,256]{2,1,0:T(8,128)} %constant.47.clone.twist_hbm), custom_call_target="tpu_custom_call" | custom-call | tf_op jit(solution)/shard_map/range_transform/pallas_call | solution.py:172
  18.5 0.6 pad_add_fusion.place_ref
  19.1 13.1 %merge_tables.1 = (bf16[8,256,512]{2,1,0:T(8,128)(2,1)}, f32[64,2,8,512]{3,2,1,0:T(8,128)}, f32[64,2,512]{2,1,0:T(2,128)}) custom-call(s32[2]{0:T(128)} %pad_add_fusion.place_ref, s32[4,16]{1,0:T(4,128)} %offsets_ref.1, s32[8,8,512]{2,1,0:T(8,128)} %bitcast.15, f32[8,8,512]{2,1,0:T(8,128)} %bitcast.16), custom_call_target="tpu_custom_call" | custom-call | tf_op jit(solution)/shard_map/merge_tables/pallas_call | solution.py:252
  32.2 12.7 %all-to-all-done = bf16[32,160,128]{2,1,0:T(8,128)(2,1)S(1)} async-done(((bf16[32,160,128]{2,1,0:T(8,128)(2,1)}), bf16[32,160,128]{2,1,0:T(8,128)(2,1)S(1)}, u32[]{:S(2)}, u32[]{:S(2)}) %all-to-all-start) | async-done | bytes 1310752 | tf_op jit(solution)/shard_map/all_to_all | solution.py:582
  44.9 0.0 copy-start
  44.9 3.6 %all-to-all-start.2 = ((bf16[32,96,128]{2,1,0:T(8,128)(2,1)}), bf16[32,96,128]{2,1,0:T(8,128)(2,1)S(1)}, u32[]{:S(2)}, u32[]{:S(2)}) async-start(bf16[32,96,128]{2,1,0:T(8,128)(2,1)} %bitcast.14), calls=%async_computation.2 | async-start | bytes 1572864 | tf_op jit(solution)/shard_map/all_to_all | solution.py:582
  48.5 0.0 copy-done
  48.5 14.0 %merged_magnitude.2 = bf16[16,80,256]{2,1,0:T(8,128)(2,1)} custom-call(bf16[16,4,80,128]{3,2,1,0:T(8,128)(2,1)} %bitcast.12, bf16[512,512]{1,0:T(8,128)(2,1)} %constant.49.clone.beam_hbm, bf16[8,256,512]{2,1,0:T(8,128)(2,1)} %get-tuple-element.21.interp_hbm, f32[64,2,8,512]{3,2,1,0:T(8,128)} %get-tuple-element.22.base_hbm, ...), custom_call_target="tpu_custom_call" | custom-call | tf_op jit(solution)/shard_map/merged_magnitude/pallas_call | solution.py:388
  62.5 6.6 %all-to-all-done.2 = bf16[32,96,128]{2,1,0:T(8,128)(2,1)S(1)} async-done(((bf16[32,96,128]{2,1,0:T(8,128)(2,1)}), bf16[32,96,128]{2,1,0:T(8,128)(2,1)S(1)}, u32[]{:S(2)}, u32[]{:S(2)}) %all-to-all-start.2) | async-done | bytes 786464 | tf_op jit(solution)/shard_map/all_to_all | solution.py:582
  69.1 0.0 copy-start.1
  69.1 3.8 %all-to-all-start.1 = ((bf16[16,80,256]{2,1,0:T(8,128)(2,1)}), bf16[16,80,256]{2,1,0:T(8,128)(2,1)S(1)}, u32[]{:S(2)}, u32[]{:S(2)}) async-start(bf16[16,80,256]{2,1,0:T(8,128)(2,1)} %merged_magnitude.2), calls=%async_computation.1 | async-start | bytes 1310720 | tf_op jit(solution)/shard_map/all_to_all | solution.py:608
  72.9 0.0 copy-done.1
  72.9 10.9 %merged_magnitude.3 = bf16[16,48,256]{2,1,0:T(8,128)(2,1)} custom-call(bf16[16,4,48,128]{3,2,1,0:T(8,128)(2,1)} %bitcast.13, bf16[512,512]{1,0:T(8,128)(2,1)} %constant.49.clone.beam_hbm, bf16[8,256,512]{2,1,0:T(8,128)(2,1)} %get-tuple-element.21.interp_hbm, f32[64,2,8,512]{3,2,1,0:T(8,128)} %get-tuple-element.22.base_hbm, ...), custom_call_target="tpu_custom_call" | custom-call | tf_op jit(solution)/shard_map/merged_magnitude/pallas_call | solution.py:388
  83.8 5.7 %all-to-all-done.1.refs_0_ = bf16[16,80,256]{2,1,0:T(8,128)(2,1)S(1)} async-done(((bf16[16,80,256]{2,1,0:T(8,128)(2,1)}), bf16[16,80,256]{2,1,0:T(8,128)(2,1)S(1)}, u32[]{:S(2)}, u32[]{:S(2)}) %all-to-all-start.1) | async-done | bytes 655392 | tf_op jit(solution)/shard_map/all_to_all | solution.py:608
  89.5 4.7 %all-to-all-start.3 = ((bf16[16,48,256]{2,1,0:T(8,128)(2,1)}), bf16[16,48,256]{2,1,0:T(8,128)(2,1)S(1)}, u32[]{:S(2)}, u32[]{:S(2)}) async-start(bf16[16,48,256]{2,1,0:T(8,128)(2,1)} %merged_magnitude.3), calls=%async_computation.3 | async-start | bytes 786432 | tf_op jit(solution)/shard_map/all_to_all | solution.py:608
  94.2 1.5 %collective-permute-start = (bf16[8,256]{1,0:T(8,128)(2,1)S(1)}, bf16[8,256]{1,0:T(8,128)(2,1)S(1)}, u32[]{:S(2)}, u32[]{:S(2)}) collective-permute-start(bf16[8,256]{1,0:T(8,128)(2,1)S(1)} %bitcast.17), channel_id=1, source_target_pairs={{0,1},{1,0},{2,3},{3,2},{4,5},{5,4},{6,7},{7,6},{8,9},{9,8},{10,11... | collective-permute-start | bytes 12296 | tf_op jit(solution)/shard_map/ppermute | solution.py:613
  95.7 2.2 %collective-permute-done.refs_1_.refs_2_ = bf16[8,256]{1,0:T(8,128)(2,1)S(1)} collective-permute-done((bf16[8,256]{1,0:T(8,128)(2,1)S(1)}, bf16[8,256]{1,0:T(8,128)(2,1)S(1)}, u32[]{:S(2)}, u32[]{:S(2)}) %collective-permute-start) | collective-permute-done | bytes 4128 | tf_op jit(solution)/shard_map/ppermute | solution.py:613
  97.9 5.7 %despeckle.2.refs_2_ = f32[256,2048]{1,0:T(8,128)} custom-call(bf16[16,80,256]{2,1,0:T(8,128)(2,1)S(1)} %all-to-all-done.1.refs_0_, bf16[8,256]{1,0:T(8,128)(2,1)S(1)} %collective-permute-done.refs_1_.refs_2_, bf16[8,256]{1,0:T(8,128)(2,1)S(1)} %collective-permute-done.refs_1_.refs_2_), custom_call_target="tpu_custom_call" | custom-call | tf_op jit(solution)/shard_map/despeckle/pallas_call | solution.py:557
  103.6 2.7 %all-to-all-done.3.refs_1_ = bf16[16,48,256]{2,1,0:T(8,128)(2,1)S(1)} async-done(((bf16[16,48,256]{2,1,0:T(8,128)(2,1)}), bf16[16,48,256]{2,1,0:T(8,128)(2,1)S(1)}, u32[]{:S(2)}, u32[]{:S(2)}) %all-to-all-start.3) | async-done | bytes 393248 | tf_op jit(solution)/shard_map/all_to_all | solution.py:608
  106.3 4.7 %despeckle.3 = f32[256,2048]{1,0:T(8,128)} custom-call(bf16[16,80,256]{2,1,0:T(8,128)(2,1)S(1)} %all-to-all-done.1.refs_0_, bf16[16,48,256]{2,1,0:T(8,128)(2,1)S(1)} %all-to-all-done.3.refs_1_, f32[256,2048]{1,0:T(8,128)} %despeckle.2.refs_2_), custom_call_target="tpu_custom_call", output_to_operand_aliasing={{}: (2, {})} | custom-call | tf_op jit(solution)/shard_map/despeckle/pallas_call | solution.py:557
  (2 shorter events, 0.0 us)
Async XLA Ops:
  5.7 39.2 %all-to-all-start = ((bf16[32,160,128]{2,1,0:T(8,128)(2,1)}), bf16[32,160,128]{2,1,0:T(8,128)(2,1)S(1)}, u32[]{:S(2)}, u32[]{:S(2)}) async-start(bf16[32,160,128]{2,1,0:T(8,128)(2,1)} %bitcast.11), calls=%async_computation | async-start | bytes 2621440 | tf_op jit(solution)/shard_map/all_to_all | solution.py:582
  44.9 3.6 %copy-start = (bf16[32,160,128]{2,1,0:T(8,128)(2,1)}, bf16[32,160,128]{2,1,0:T(8,128)(2,1)S(1)}, u32[]{:S(2)}) copy-start(bf16[32,160,128]{2,1,0:T(8,128)(2,1)S(1)} %all-to-all-done) | copy-start | bytes 3932164
  44.9 24.2 %all-to-all-start.2 = ((bf16[32,96,128]{2,1,0:T(8,128)(2,1)}), bf16[32,96,128]{2,1,0:T(8,128)(2,1)S(1)}, u32[]{:S(2)}, u32[]{:S(2)}) async-start(bf16[32,96,128]{2,1,0:T(8,128)(2,1)} %bitcast.14), calls=%async_computation.2 | async-start | bytes 1572864 | tf_op jit(solution)/shard_map/all_to_all | solution.py:582
  69.1 3.8 %copy-start.1 = (bf16[32,96,128]{2,1,0:T(8,128)(2,1)}, bf16[32,96,128]{2,1,0:T(8,128)(2,1)S(1)}, u32[]{:S(2)}) copy-start(bf16[32,96,128]{2,1,0:T(8,128)(2,1)S(1)} %all-to-all-done.2) | copy-start | bytes 2359300
  69.1 20.4 %all-to-all-start.1 = ((bf16[16,80,256]{2,1,0:T(8,128)(2,1)}), bf16[16,80,256]{2,1,0:T(8,128)(2,1)S(1)}, u32[]{:S(2)}, u32[]{:S(2)}) async-start(bf16[16,80,256]{2,1,0:T(8,128)(2,1)} %merged_magnitude.2), calls=%async_computation.1 | async-start | bytes 1310720 | tf_op jit(solution)/shard_map/all_to_all | solution.py:608
  89.5 16.8 %all-to-all-start.3 = ((bf16[16,48,256]{2,1,0:T(8,128)(2,1)}), bf16[16,48,256]{2,1,0:T(8,128)(2,1)S(1)}, u32[]{:S(2)}, u32[]{:S(2)}) async-start(bf16[16,48,256]{2,1,0:T(8,128)(2,1)} %merged_magnitude.3), calls=%async_computation.3 | async-start | bytes 786432 | tf_op jit(solution)/shard_map/all_to_all | solution.py:608
  94.2 3.7 %collective-permute-start = (bf16[8,256]{1,0:T(8,128)(2,1)S(1)}, bf16[8,256]{1,0:T(8,128)(2,1)S(1)}, u32[]{:S(2)}, u32[]{:S(2)}) collective-permute-start(bf16[8,256]{1,0:T(8,128)(2,1)S(1)} %bitcast.17), channel_id=1, source_target_pairs={{0,1},{1,0},{2,3},{3,2},{4,5},{5,4},{6,7},{7,6},{8,9},{9,8},{10,11... | collective-permute-start | bytes 12296 | tf_op jit(solution)/shard_map/ppermute | solution.py:613

commit v5 on v4

--- a/solution.py
+++ b/solution.py
@@ -109,7 +109,7 @@
     pulses = raw_ref.shape[1]
     blocks = raw_sems.shape[0]
     block = pulses // blocks
-    pair = 2
+    pair = 4
 
     def fetch(i):
         rows = pl.ds(pl.multiple_of(i * block, block), block)
@@ -182,7 +182,7 @@
             pltpu.VMEM(shape, jnp.bfloat16),
             pltpu.SemaphoreType.DMA((pulses // (2 * ROWS),)),
             pltpu.SemaphoreType.DMA((2,)),
-            pltpu.SemaphoreType.DMA((GROUP // 2,)),
+            pltpu.SemaphoreType.DMA((GROUP // 4,)),
         ],
         compiler_params=pltpu.CompilerParams(vmem_limit_bytes=VMEM_BYTES),
         name="range_transform",

time: 112 us -> 111 us (level)
  Pallas kernels: 59.5 us -> 58 us
    pallas_call x2, Pallas kernels: 11.1 us -> 9.6 us  [range_transform(): pl.pallas_call(transform_kernel, in_specs=[ANY, ANY, ANY], out_specs=ANY,...]
where the time goes in v5:
time: 111 us; the launch traced here: 110 us
  Pallas kernels  58 us (52%)
  waiting for transfers between devices  30.6 us (28%)
  starting transfers between devices  20.9 us (19%)
    pallas_call x2, Pallas kernels, merged_magnitude(): pl.pallas_call(functools.partial(merge_kernel, segments), in_specs=[ANY]...  24.8 us
    all_to_all x2, waiting for transfers between devices, regroup(): lax.all_to_all(block, ('sub', 'rng'), split_axis=0, concat_axis=0, tiled=...  20 us
    pallas_call x1, Pallas kernels, merge_tables(): pl.pallas_call(tables_kernel, in_specs=[SMEM, SMEM, VMEM, VMEM], out_shap...  13.1 us
    all_to_all x2, starting transfers between devices, regroup(): lax.all_to_all(block, ('sub', 'rng'), split_axis=0, concat_axis=0, tiled=...  11 us
    pallas_call x2, Pallas kernels, despeckle(): pl.pallas_call(functools.partial(diffuse_kernel, zones, len(cells)), in_s...  10.5 us
    pallas_call x2, Pallas kernels, range_transform(): pl.pallas_call(transform_kernel, in_specs=[ANY, ANY, ANY], out_specs=ANY,...  9.6 us
    all_to_all x2, starting transfers between devices, per_device(): lax.all_to_all(magnitude, 'sub', split_axis=0, concat_axis=0, tiled=True,...  8.48 us
    all_to_all x2, waiting for transfers between devices, per_device(): lax.all_to_all(magnitude, 'sub', split_axis=0, concat_axis=0, tiled=True,...  8.37 us
  transfers between devices with their start and end apart: 5, of which 5 were waited for; matrix products, arithmetic and copies ran while one was open for 1% of the time, Pallas kernels for 44%

profile of v5, /device:TPU:0, one launch (start us, length us, event | category | flops | bytes accessed | tf_op | source)
XLA Modules:
  0.0 110.3 jit_solution(13070392644014692486)
XLA Ops:
  0.0 4.9 %range_transform.2 = bf16[16,320,128]{2,1,0:T(8,128)(2,1)} custom-call(bf16[2,128,4096]{2,1,0:T(8,128)(2,1)} %raw_hbm.2, bf16[320,512]{1,0:T(8,128)(2,1)} %constant.46.clone.matrix_hbm, f32[2,16,256]{2,1,0:T(8,128)} %constant.47.clone.twist_hbm), custom_call_target="tpu_custom_call" | custom-call | tf_op jit(solution)/shard_map/range_transform/pallas_call | solution.py:172
  4.9 7.3 %all-to-all-start = ((bf16[32,160,128]{2,1,0:T(8,128)(2,1)}), bf16[32,160,128]{2,1,0:T(8,128)(2,1)S(1)}, u32[]{:S(2)}, u32[]{:S(2)}) async-start(bf16[32,160,128]{2,1,0:T(8,128)(2,1)} %bitcast.11), calls=%async_computation | async-start | bytes 2621440 | tf_op jit(solution)/shard_map/all_to_all | solution.py:582
  12.3 4.7 %range_transform.3 = bf16[16,192,128]{2,1,0:T(8,128)(2,1)} custom-call(bf16[2,128,4096]{2,1,0:T(8,128)(2,1)} %raw_hbm.2, bf16[192,512]{1,0:T(8,128)(2,1)} %constant.48.clone.matrix_hbm, f32[2,16,256]{2,1,0:T(8,128)} %constant.47.clone.twist_hbm), custom_call_target="tpu_custom_call" | custom-call | tf_op jit(solution)/shard_map/range_transform/pallas_call | solution.py:172
  17.0 0.6 pad_add_fusion.place_ref
  17.6 13.1 %merge_tables.1 = (bf16[8,256,512]{2,1,0:T(8,128)(2,1)}, f32[64,2,8,512]{3,2,1,0:T(8,128)}, f32[64,2,512]{2,1,0:T(2,128)}) custom-call(s32[2]{0:T(128)} %pad_add_fusion.place_ref, s32[4,16]{1,0:T(4,128)} %offsets_ref.1, s32[8,8,512]{2,1,0:T(8,128)} %bitcast.15, f32[8,8,512]{2,1,0:T(8,128)} %bitcast.16), custom_call_target="tpu_custom_call" | custom-call | tf_op jit(solution)/shard_map/merge_tables/pallas_call | solution.py:252
  30.7 13.4 %all-to-all-done = bf16[32,160,128]{2,1,0:T(8,128)(2,1)S(1)} async-done(((bf16[32,160,128]{2,1,0:T(8,128)(2,1)}), bf16[32,160,128]{2,1,0:T(8,128)(2,1)S(1)}, u32[]{:S(2)}, u32[]{:S(2)}) %all-to-all-start) | async-done | bytes 1310752 | tf_op jit(solution)/shard_map/all_to_all | solution.py:582
  44.1 0.0 copy-start
  44.1 3.6 %all-to-all-start.2 = ((bf16[32,96,128]{2,1,0:T(8,128)(2,1)}), bf16[32,96,128]{2,1,0:T(8,128)(2,1)S(1)}, u32[]{:S(2)}, u32[]{:S(2)}) async-start(bf16[32,96,128]{2,1,0:T(8,128)(2,1)} %bitcast.14), calls=%async_computation.2 | async-start | bytes 1572864 | tf_op jit(solution)/shard_map/all_to_all | solution.py:582
  47.7 0.0 copy-done
  47.7 14.0 %merged_magnitude.2 = bf16[16,80,256]{2,1,0:T(8,128)(2,1)} custom-call(bf16[16,4,80,128]{3,2,1,0:T(8,128)(2,1)} %bitcast.12, bf16[512,512]{1,0:T(8,128)(2,1)} %constant.49.clone.beam_hbm, bf16[8,256,512]{2,1,0:T(8,128)(2,1)} %get-tuple-element.21.interp_hbm, f32[64,2,8,512]{3,2,1,0:T(8,128)} %get-tuple-element.22.base_hbm, ...), custom_call_target="tpu_custom_call" | custom-call | tf_op jit(solution)/shard_map/merged_magnitude/pallas_call | solution.py:388
  61.7 6.6 %all-to-all-done.2 = bf16[32,96,128]{2,1,0:T(8,128)(2,1)S(1)} async-done(((bf16[32,96,128]{2,1,0:T(8,128)(2,1)}), bf16[32,96,128]{2,1,0:T(8,128)(2,1)S(1)}, u32[]{:S(2)}, u32[]{:S(2)}) %all-to-all-start.2) | async-done | bytes 786464 | tf_op jit(solution)/shard_map/all_to_all | solution.py:582
  68.3 0.0 copy-start.1
  68.3 3.8 %all-to-all-start.1 = ((bf16[16,80,256]{2,1,0:T(8,128)(2,1)}), bf16[16,80,256]{2,1,0:T(8,128)(2,1)S(1)}, u32[]{:S(2)}, u32[]{:S(2)}) async-start(bf16[16,80,256]{2,1,0:T(8,128)(2,1)} %merged_magnitude.2), calls=%async_computation.1 | async-start | bytes 1310720 | tf_op jit(solution)/shard_map/all_to_all | solution.py:608
  72.1 0.0 copy-done.1
  72.1 10.9 %merged_magnitude.3 = bf16[16,48,256]{2,1,0:T(8,128)(2,1)} custom-call(bf16[16,4,48,128]{3,2,1,0:T(8,128)(2,1)} %bitcast.13, bf16[512,512]{1,0:T(8,128)(2,1)} %constant.49.clone.beam_hbm, bf16[8,256,512]{2,1,0:T(8,128)(2,1)} %get-tuple-element.21.interp_hbm, f32[64,2,8,512]{3,2,1,0:T(8,128)} %get-tuple-element.22.base_hbm, ...), custom_call_target="tpu_custom_call" | custom-call | tf_op jit(solution)/shard_map/merged_magnitude/pallas_call | solution.py:388
  83.0 5.7 %all-to-all-done.1.refs_0_ = bf16[16,80,256]{2,1,0:T(8,128)(2,1)S(1)} async-done(((bf16[16,80,256]{2,1,0:T(8,128)(2,1)}), bf16[16,80,256]{2,1,0:T(8,128)(2,1)S(1)}, u32[]{:S(2)}, u32[]{:S(2)}) %all-to-all-start.1) | async-done | bytes 655392 | tf_op jit(solution)/shard_map/all_to_all | solution.py:608
  88.7 4.7 %all-to-all-start.3 = ((bf16[16,48,256]{2,1,0:T(8,128)(2,1)}), bf16[16,48,256]{2,1,0:T(8,128)(2,1)S(1)}, u32[]{:S(2)}, u32[]{:S(2)}) async-start(bf16[16,48,256]{2,1,0:T(8,128)(2,1)} %merged_magnitude.3), calls=%async_computation.3 | async-start | bytes 786432 | tf_op jit(solution)/shard_map/all_to_all | solution.py:608
  93.4 1.5 %collective-permute-start = (bf16[8,256]{1,0:T(8,128)(2,1)S(1)}, bf16[8,256]{1,0:T(8,128)(2,1)S(1)}, u32[]{:S(2)}, u32[]{:S(2)}) collective-permute-start(bf16[8,256]{1,0:T(8,128)(2,1)S(1)} %bitcast.17), channel_id=1, source_target_pairs={{0,1},{1,0},{2,3},{3,2},{4,5},{5,4},{6,7},{7,6},{8,9},{9,8},{10,11... | collective-permute-start | bytes 12296 | tf_op jit(solution)/shard_map/ppermute | solution.py:613
  94.9 2.2 %collective-permute-done.refs_1_.refs_2_ = bf16[8,256]{1,0:T(8,128)(2,1)S(1)} collective-permute-done((bf16[8,256]{1,0:T(8,128)(2,1)S(1)}, bf16[8,256]{1,0:T(8,128)(2,1)S(1)}, u32[]{:S(2)}, u32[]{:S(2)}) %collective-permute-start) | collective-permute-done | bytes 4128 | tf_op jit(solution)/shard_map/ppermute | solution.py:613
  97.1 5.7 %despeckle.2.refs_2_ = f32[256,2048]{1,0:T(8,128)} custom-call(bf16[16,80,256]{2,1,0:T(8,128)(2,1)S(1)} %all-to-all-done.1.refs_0_, bf16[8,256]{1,0:T(8,128)(2,1)S(1)} %collective-permute-done.refs_1_.refs_2_, bf16[8,256]{1,0:T(8,128)(2,1)S(1)} %collective-permute-done.refs_1_.refs_2_), custom_call_target="tpu_custom_call" | custom-call | tf_op jit(solution)/shard_map/despeckle/pallas_call | solution.py:557
  102.8 2.7 %all-to-all-done.3.refs_1_ = bf16[16,48,256]{2,1,0:T(8,128)(2,1)S(1)} async-done(((bf16[16,48,256]{2,1,0:T(8,128)(2,1)}), bf16[16,48,256]{2,1,0:T(8,128)(2,1)S(1)}, u32[]{:S(2)}, u32[]{:S(2)}) %all-to-all-start.3) | async-done | bytes 393248 | tf_op jit(solution)/shard_map/all_to_all | solution.py:608
  105.5 4.7 %despeckle.3 = f32[256,2048]{1,0:T(8,128)} custom-call(bf16[16,80,256]{2,1,0:T(8,128)(2,1)S(1)} %all-to-all-done.1.refs_0_, bf16[16,48,256]{2,1,0:T(8,128)(2,1)S(1)} %all-to-all-done.3.refs_1_, f32[256,2048]{1,0:T(8,128)} %despeckle.2.refs_2_), custom_call_target="tpu_custom_call", output_to_operand_aliasing={{}: (2, {})} | custom-call | tf_op jit(solution)/shard_map/despeckle/pallas_call | solution.py:557
  (2 shorter events, 0.0 us)
Async XLA Ops:
  4.9 39.2 %all-to-all-start = ((bf16[32,160,128]{2,1,0:T(8,128)(2,1)}), bf16[32,160,128]{2,1,0:T(8,128)(2,1)S(1)}, u32[]{:S(2)}, u32[]{:S(2)}) async-start(bf16[32,160,128]{2,1,0:T(8,128)(2,1)} %bitcast.11), calls=%async_computation | async-start | bytes 2621440 | tf_op jit(solution)/shard_map/all_to_all | solution.py:582
  44.1 3.6 %copy-start = (bf16[32,160,128]{2,1,0:T(8,128)(2,1)}, bf16[32,160,128]{2,1,0:T(8,128)(2,1)S(1)}, u32[]{:S(2)}) copy-start(bf16[32,160,128]{2,1,0:T(8,128)(2,1)S(1)} %all-to-all-done) | copy-start | bytes 3932164
  44.1 24.2 %all-to-all-start.2 = ((bf16[32,96,128]{2,1,0:T(8,128)(2,1)}), bf16[32,96,128]{2,1,0:T(8,128)(2,1)S(1)}, u32[]{:S(2)}, u32[]{:S(2)}) async-start(bf16[32,96,128]{2,1,0:T(8,128)(2,1)} %bitcast.14), calls=%async_computation.2 | async-start | bytes 1572864 | tf_op jit(solution)/shard_map/all_to_all | solution.py:582
  68.3 3.8 %copy-start.1 = (bf16[32,96,128]{2,1,0:T(8,128)(2,1)}, bf16[32,96,128]{2,1,0:T(8,128)(2,1)S(1)}, u32[]{:S(2)}) copy-start(bf16[32,96,128]{2,1,0:T(8,128)(2,1)S(1)} %all-to-all-done.2) | copy-start | bytes 2359300
  68.3 20.4 %all-to-all-start.1 = ((bf16[16,80,256]{2,1,0:T(8,128)(2,1)}), bf16[16,80,256]{2,1,0:T(8,128)(2,1)S(1)}, u32[]{:S(2)}, u32[]{:S(2)}) async-start(bf16[16,80,256]{2,1,0:T(8,128)(2,1)} %merged_magnitude.2), calls=%async_computation.1 | async-start | bytes 1310720 | tf_op jit(solution)/shard_map/all_to_all | solution.py:608
  88.7 16.8 %all-to-all-start.3 = ((bf16[16,48,256]{2,1,0:T(8,128)(2,1)}), bf16[16,48,256]{2,1,0:T(8,128)(2,1)S(1)}, u32[]{:S(2)}, u32[]{:S(2)}) async-start(bf16[16,48,256]{2,1,0:T(8,128)(2,1)} %merged_magnitude.3), calls=%async_computation.3 | async-start | bytes 786432 | tf_op jit(solution)/shard_map/all_to_all | solution.py:608
  93.4 3.7 %collective-permute-start = (bf16[8,256]{1,0:T(8,128)(2,1)S(1)}, bf16[8,256]{1,0:T(8,128)(2,1)S(1)}, u32[]{:S(2)}, u32[]{:S(2)}) collective-permute-start(bf16[8,256]{1,0:T(8,128)(2,1)S(1)} %bitcast.17), channel_id=1, source_target_pairs={{0,1},{1,0},{2,3},{3,2},{4,5},{5,4},{6,7},{7,6},{8,9},{9,8},{10,11... | collective-permute-start | bytes 12296 | tf_op jit(solution)/shard_map/ppermute | solution.py:613
